TPU v7x, 32 devices: a whole 2x2x4 slice. The times are simulated.
32 devices in a mesh: groups: 2 (over x), ctx: 16 (over z, y, core).
Axes of the slice: x: 2, y: 2, z: 4, core: 2. Of those that a mesh axis runs over, the one named last changes fastest.
Arguments:
- queries: bfloat16 [96, 4096], P(('groups', 'ctx')), parts along dimension 0, may hold values from -200 to 200
- cache_keys: bfloat16 [4096, 512], P(('groups', 'ctx')), parts along dimension 0, may hold values from -6 to 6
- cache_values: bfloat16 [4096, 512], P(('groups', 'ctx')), parts along dimension 0, may hold values from -6 to 6
- new_keys: bfloat16 [96, 512], P(('groups', 'ctx')), parts along dimension 0, may hold values from -6 to 6
- new_values: bfloat16 [96, 512], P(('groups', 'ctx')), parts along dimension 0, may hold values from -6 to 6
- cache_lengths: int32 [32], P(('groups', 'ctx')), parts along dimension 0, may hold values from 0 to 128, as said below
- residual_in: bfloat16 [96, 2048], P(('groups', 'ctx')), parts along dimension 0, may hold values from -6 to 6
- out_weight: bfloat16 [4096, 2048], P('ctx'), may hold values from -3 to 3
- norm_gain: bfloat16 [2048], replicated, may hold values from 0.25 to 1.75
- expert_gate: bfloat16 [16, 2048, 768], P('ctx'), may hold values from -0.125 to 0.125
- expert_up: bfloat16 [16, 2048, 768], P('ctx'), may hold values from -0.125 to 0.125
- expert_down: bfloat16 [16, 768, 2048], P('ctx'), may hold values from -0.21875 to 0.21875
- expert_ids: int32 [96, 8], P(('groups', 'ctx')), parts along dimension 0, may hold values from 0 to 15, all different within a row; in each aligned block of 3 rows (0 to 2, 3 to 5, ...) at most 3 rows name the same one
- expert_weights: float32 [96, 8], P(('groups', 'ctx')), parts along dimension 0, may hold values from 0.03 to 0.4
Outputs:
- layer_out: bfloat16 [96, 2048], P(('groups', 'ctx')), parts along dimension 0
There are 2 independent parts, one for each index of `groups`. A program takes and returns all parts, laid end to end along the dimension named above; an argument that names none is the same for every part. Nothing has to cross between parts.
Inputs may be any that keep to these rules, and one draw needn't show every extreme that they name: `cache_lengths`: some shard in every draw is full, with 128 live positions. `expert_ids`: within one block of 3 rows no expert is named more than 3 times, a bound that some block reaches.
All inputs are finite; a program needn't handle non-finite values.
Results may differ from a plain program's by a relative error of at most 0.01.
Values may be sent and summed in bfloat16 or wider, within the bound.
No kernel may reach another device: no remote copies, remote signals or barrier semaphores. Data moves between devices by JAX's collectives and lax.ppermute only.
A program may use at most 64 MiB of HBM per device.

v0:
```python
import functools

import jax
import jax.numpy as jnp
from jax import lax
from jax.experimental import pallas as pl
from jax.experimental.pallas import tpu as pltpu
from jax.sharding import PartitionSpec as P


HEADS = 32
KV_HEADS = 4
HEAD_DIM = 128
GROUP = HEADS // KV_HEADS
LANES = 128

MASKED = -1e30
epsilon = 1e-06

f32, bf16 = jnp.float32, jnp.bfloat16
VMEM = pl.BlockSpec(memory_space=pltpu.VMEM)


def coordinates(inner):
    device = lax.axis_index("ctx")
    return device // inner, lax.rem(device, inner)


def call(body, outs, operands, scratch=(), grant=4, flops=10**9):
    return pl.pallas_call(
        body,
        out_shape=outs,
        in_specs=[VMEM] * len(operands),
        out_specs=jax.tree.map(lambda _: VMEM, outs),
        scratch_shapes=list(scratch),
        compiler_params=pltpu.CompilerParams(vmem_limit_bytes=grant << 20),
        cost_estimate=pl.CostEstimate(flops=flops, bytes_accessed=10**6, transcendentals=0),
    )(*operands)


def third(x, rows):
    return jnp.right_shift(x * (-(-65536 // rows)), 16)


def owners(position, half, rows):
    odd = (position >= half).astype(jnp.int32)
    rest = position - odd * half
    pair = third(rest, rows)
    return 2 * pair + odd, rest - pair * rows


def place(shard, half, rows):
    return jnp.bitwise_and(shard, 1) * half + jnp.right_shift(shard, 1) * rows


def aligned(index, size):
    return pl.ds(pl.multiple_of(index * size, size), size)


def pack_span(outer, inner, rows, lines, token, lengths, new_keys, new_values, queries, ids, weights, *refs):
    outs, (wide, routing) = refs[:outer], refs[outer:]
    a, _ = coordinates(inner)
    per_row = rows * GROUP
    live = lengths[...].astype(f32).reshape(1, 1)
    wide[...] = jnp.zeros_like(wide)
    wide[per_row + 2 * rows : per_row + 2 * rows + 1] = jnp.broadcast_to(live, (1, HEAD_DIM))
    weight = weights[...]
    high = weight.astype(bf16).astype(f32)
    routing[...] = jnp.zeros_like(routing)
    for i, part in enumerate((ids[...].astype(f32), high, weight - high)):
        routing[8 * i : 8 * i + rows] = part
    top = ids.shape[1]
    lane = lax.broadcasted_iota(jnp.int32, (top, HEAD_DIM), 1)
    turn = lax.broadcasted_iota(jnp.int32, (top, HEAD_DIM), 0)
    copies = jnp.where(lax.rem(lane, top) == turn, 1.0, 0.0).astype(bf16)
    repeated = jnp.dot(routing[...].astype(bf16), copies, preferred_element_type=f32)
    lane = lax.broadcasted_iota(jnp.int32, (8, HEAD_DIM), 1)
    row = lax.broadcasted_iota(jnp.int32, (8, HEAD_DIM), 0)
    inside = (lane >= row * top) & (lane < row * top + top)
    for i in range(3):
        wide[lines + i : lines + i + 1] = jnp.sum(
            jnp.where(inside, repeated[8 * i : 8 * i + 8], 0.0), axis=0, keepdims=True
        )
    for k in range(outer):
        head = jnp.bitwise_xor(a, k)
        lanes = aligned(head, HEAD_DIM)
        block = queries[:, aligned(head, GROUP * HEAD_DIM)].astype(f32)
        for g in range(GROUP):
            wide[g * rows : (g + 1) * rows] = block[:, g * HEAD_DIM : (g + 1) * HEAD_DIM]
        wide[per_row : per_row + rows] = new_keys[:, lanes].astype(f32)
        wide[per_row + rows : per_row + 2 * rows] = new_values[:, lanes].astype(f32)
        outs[k][...] = wide[...].astype(bf16)


def pack_cache(outer, inner, keys, values, *outs):
    a, _ = coordinates(inner)
    cache = keys.shape[0]
    for k in range(outer):
        lanes = aligned(jnp.bitwise_xor(a, k), HEAD_DIM)
        outs[k][0:cache] = keys[:, lanes]
        outs[k][cache:] = values[:, lanes]


def plan(outer, inner, rows, count, pick, token):
    a, b = coordinates(inner)
    per_row = rows * GROUP
    position = lax.broadcasted_iota(jnp.int32, (count, 1), 0)
    owner, row = owners(position, count // 2, rows)
    at_a = jnp.bitwise_xor(jnp.right_shift(owner, inner.bit_length() - 1), a)
    at_b = jnp.bitwise_xor(jnp.bitwise_and(owner, inner - 1), b)
    source = (at_b * outer + at_a) * per_row + row
    source = jnp.where(owner < outer * inner, source, -per_row)
    column = lax.broadcasted_iota(jnp.int32, (count, pick.shape[1]), 1)
    for g in range(GROUP):
        pick[g * count : (g + 1) * count] = jnp.where(
            column == source + g * rows, 1.0, 0.0
        ).astype(bf16)
    token[...] = jnp.zeros_like(token)


def collect(outer, rows, lines, *refs):
    spans, out, wide = refs[:outer], refs[outer], refs[outer + 1]
    per_row = rows * GROUP
    for k in range(outer):
        block = spans[k][...].astype(f32)
        wide[k * per_row : (k + 1) * per_row] = block[0:per_row]
        for i in range(3):
            at = outer * per_row + i * outer + k
            wide[at : at + 1] = block[lines + i : lines + i + 1]
    out[...] = wide[...].astype(bf16)


def attend(outer, inner, rows, lines, count, heads, step, *refs):
    pick, spans, caches = refs[0], refs[1 : outer + 1], refs[outer + 1 : 2 * outer + 1]
    queries, refs = refs[2 * outer + 1 : 2 * outer + 1 + inner], refs[2 * outer + 1 + inner :]
    outs, (fresh, parts) = refs[:inner], refs[inner:]
    a, b = coordinates(inner)
    cache = caches[0].shape[0] // 2
    per_row = rows * GROUP
    gathered = jnp.concatenate([block[0 : outer * per_row] for block in queries], 0)
    wanted = jnp.dot(pick[...], gathered, preferred_element_type=f32).astype(bf16)

    def score(keys, usable):
        s = lax.dot_general(
            wanted, keys, (((1,), (1,)), ((), ())), preferred_element_type=f32
        ) * HEAD_DIM ** (-0.5)
        return jnp.where(usable, s.reshape((GROUP, count, keys.shape[0])), MASKED)

    fresh[...] = jnp.zeros_like(fresh)
    owner, row = owners(lax.broadcasted_iota(jnp.int32, (count, 1), 0), count // 2, rows)
    position = owner * rows + row
    slot = lax.broadcasted_iota(jnp.int32, (count, outer * lines), 1)
    reach = jnp.full((count, outer * lines), -1, jnp.int32)
    lives = []
    for k in range(outer):
        block = spans[k][0:lines].astype(f32)
        lives.append(block[per_row + 2 * rows : per_row + 2 * rows + 1, 0:1])
        first = k * lines + per_row
        fresh[first : first + rows] = block[per_row + rows : per_row + 2 * rows]
        start = rows * (jnp.bitwise_xor(a, k) * inner + b)
        inside = (slot >= first) & (slot < first + rows)
        reach = jnp.where(inside, position - start - (slot - first), reach)
    keys = [jnp.concatenate([block[0:lines] for block in spans], 0)]
    values = [fresh[...].astype(bf16)]
    usable = [(reach >= 0)[None]]
    index = lax.broadcasted_iota(jnp.int32, (count, cache), 1).astype(f32)
    for k in range(outer):
        keys.append(caches[k][0:cache])
        values.append(caches[k][cache:])
        usable.append(((lives[k] - index) > 0.0)[None])
    scores = [score(key, ok) for key, ok in zip(keys, usable)]
    largest = functools.reduce(
        jnp.maximum, [jnp.max(s, axis=-1, keepdims=True) for s in scores]
    )
    largest = largest.astype(bf16).astype(f32)
    total = jnp.zeros((GROUP, count, 1), f32)
    summed = jnp.zeros((GROUP * count, HEAD_DIM), f32)
    for s, ok, value in zip(scores, usable, values):
        e = jnp.where(ok, jnp.exp(s - largest), 0.0)
        total = total + jnp.sum(e, axis=-1, keepdims=True)
        summed = summed + jnp.dot(
            e.reshape(GROUP * count, value.shape[0]).astype(bf16),
            value,
            preferred_element_type=f32,
        )
    total = total.reshape(GROUP * count, 1)
    high = total.astype(bf16).astype(f32)
    lane = lax.broadcasted_iota(jnp.int32, (GROUP * count, HEAD_DIM), 1)
    stats = jnp.where(
        lane == 0,
        largest.reshape(GROUP * count, 1),
        jnp.where(lane == 1, high, total - high),
    )
    parts[:, 0:HEAD_DIM] = summed.astype(bf16)
    parts[:, HEAD_DIM:] = stats.astype(bf16)
    for k in range(inner):
        first = jnp.right_shift(jnp.bitwise_xor(b, k) * step, HEAD_DIM.bit_length() - 1)
        outs[k][...] = parts[pl.ds(pl.multiple_of(first * count, 16), heads * count)]


def project(inner, rows, count, heads, *refs):
    chunks, (weight, residual), refs = refs[:inner], refs[inner : inner + 2], refs[inner + 2 :]
    own, outs, total = refs[0], refs[1:inner], refs[inner]
    _, b = coordinates(inner)
    stats = [chunk[:, HEAD_DIM:].astype(f32) for chunk in chunks]
    largest = functools.reduce(jnp.maximum, [s[:, 0:1] for s in stats])
    scales = [jnp.exp(s[:, 0:1] - largest) for s in stats]
    denominator = sum(w * (s[:, 1:2] + s[:, 2:3]) for w, s in zip(scales, stats))
    joined = sum(
        chunk[:, 0:HEAD_DIM].astype(f32) * (w / denominator)
        for w, chunk in zip(scales, chunks)
    ).astype(bf16)
    total[...] = sum(
        jnp.dot(
            joined[h * count : (h + 1) * count],
            weight[h * HEAD_DIM : (h + 1) * HEAD_DIM],
            preferred_element_type=f32,
        )
        for h in range(heads)
    )
    start = place(lax.axis_index("ctx"), count // 2, rows)
    added = residual[...].astype(f32)
    for r in range(rows):
        row = pl.ds(start + r, 1)
        total[row] = total[row] + added[r : r + 1]
    columns = own.shape[1]
    own[...] = total[:, aligned(b, columns)]
    for k in range(1, inner):
        outs[k - 1][...] = total[:, aligned(jnp.bitwise_xor(b, k), columns)].astype(bf16)


def add_up(own, *refs):
    others, (kept, sent) = refs[:-2], refs[-2:]
    partial = own[...]
    for other in others:
        partial = partial + other[...].astype(f32)
    kept[...] = partial
    sent[...] = partial.astype(bf16)


def route(outer, inner, rows, count, top, *refs):
    blocks, out = refs[:-1], refs[-1]
    a, b = coordinates(inner)
    expert = lax.axis_index("ctx").astype(f32)
    lane = lax.broadcasted_iota(jnp.int32, (outer, HEAD_DIM), 1)
    for m in range(inner):
        info = blocks[m][outer * rows * GROUP :].astype(f32)
        named, high, low = (info[i * outer : (i + 1) * outer] for i in range(3))
        weight = jnp.where(named == expert, high + low, 0.0)
        for r in range(rows):
            inside = (lane >= r * top) & (lane < r * top + top)
            share = jnp.sum(jnp.where(inside, weight, 0.0), axis=1, keepdims=True)
            share = jnp.broadcast_to(share, (outer, LANES))
            for k in range(outer):
                shard = jnp.bitwise_xor(a, k) * inner + jnp.bitwise_xor(b, m)
                out[pl.ds(place(shard, count // 2, rows) + r, 1)] = share[k : k + 1]


def expert(inner, rows, gate, up, down, gain, weights, *refs):
    pieces, (kept, sent, mine, state, normed, held) = refs[:inner], refs[inner:]
    _, b = coordinates(inner)
    columns = pieces[0].shape[1]
    half = kept.shape[0]
    values = [piece[...].astype(f32) for piece in pieces]
    squares = sum(jnp.sum(v * v, axis=1, keepdims=True) for v in values)
    scale = lax.rsqrt(squares * (1.0 / (inner * columns)) + epsilon)
    for k, value in enumerate(values):
        lanes = aligned(jnp.bitwise_xor(b, k), columns)
        state[:, lanes] = value
        normed[:, lanes] = (value * scale * gain[:, lanes].astype(f32)).astype(bf16)
    start = place(lax.axis_index("ctx"), half, rows)
    for r in range(rows):
        mine[r : r + 1] = state[pl.ds(start + r, 1)]
    x = normed[...]
    gated = jnp.dot(x, gate[0], preferred_element_type=f32)
    lifted = jnp.dot(x, up[0], preferred_element_type=f32)
    active = (gated / (1.0 + jnp.exp(-gated)) * lifted).astype(bf16)
    held[...] = jnp.dot(active, down[0], preferred_element_type=f32) * weights[:, 0:1]
    odd = jnp.bitwise_and(b, 1)
    kept[...] = held[aligned(odd, half)]
    sent[...] = held[aligned(1 - odd, half)].astype(bf16)


def join(rows, kept, other, out, total, dense):
    total[...] = kept[...] + other[...].astype(f32)
    for t in range(out.shape[0]):
        for j in range(total.shape[1] // LANES):
            dense[t, j * rows : (j + 1) * rows] = total[
                t * rows : (t + 1) * rows, j * LANES : (j + 1) * LANES
            ]
    out[...] = dense[...].astype(bf16)


def combine(rows, state, back, out, total):
    total[...] = sum(back[t].astype(f32) for t in range(back.shape[0]))
    for j in range(state.shape[1] // LANES):
        lanes = slice(j * LANES, (j + 1) * LANES)
        out[:, lanes] = (state[:, lanes] + total[j * rows : (j + 1) * rows]).astype(bf16)


def local(
    queries,
    cache_keys,
    cache_values,
    new_keys,
    new_values,
    cache_lengths,
    residual_in,
    out_weight,
    norm_gain,
    expert_gate,
    expert_up,
    expert_down,
    expert_ids,
    expert_weights,
):
    shards = lax.axis_size("ctx")
    outer = KV_HEADS
    inner = shards // outer
    rows, width = residual_in.shape
    cache = cache_keys.shape[0]
    half = -(-shards // 2 * rows // 8) * 8
    count = 2 * half
    top = expert_ids.shape[1]
    step = out_weight.shape[0]
    heads = max(1, step // HEAD_DIM)
    columns = width // inner
    lines = rows * width // LANES

    def shape(dims, dtype=bf16):
        return jax.ShapeDtypeStruct(dims, dtype)

    def outward(x, k):
        pairs = [(i, ((i // inner) ^ k) * inner + i % inner) for i in range(shards)]
        return lax.ppermute(x, "ctx", pairs)

    def inward(x, k):
        pairs = [(i, i // inner * inner + ((i % inner) ^ k)) for i in range(shards)]
        return lax.ppermute(x, "ctx", pairs)

    def exchange(move, blocks):
        moved = [blocks[0]]
        for k in range(1, len(blocks)):
            moved.append(move(blocks[k], k))
        return moved

    per_row = rows * GROUP
    span_lines = -(-(per_row + 2 * rows + 1) // 16) * 16
    asked_lines = outer * per_row + -(-3 * outer // 8) * 8
    pick, token = call(
        functools.partial(plan, outer, inner, rows, count),
        [shape((GROUP * count, shards * per_row)), shape((8, LANES), f32)],
        (),
        grant=max(4, count // 12),
    )
    spans = call(
        functools.partial(pack_span, outer, inner, rows, span_lines),
        [shape((span_lines + 8, HEAD_DIM))] * outer,
        (token, cache_lengths, new_keys, new_values, queries, expert_ids, expert_weights),
        [pltpu.VMEM((span_lines + 8, HEAD_DIM), f32), pltpu.VMEM((24, top), f32)],
    )
    spans = exchange(outward, spans)
    caches = call(
        functools.partial(pack_cache, outer, inner),
        [shape((2 * cache, HEAD_DIM))] * outer,
        (cache_keys, cache_values),
    )
    caches = exchange(outward, caches)
    wanted = call(
        functools.partial(collect, outer, rows, span_lines),
        shape((asked_lines, HEAD_DIM)),
        spans,
        [pltpu.VMEM((asked_lines, HEAD_DIM), f32)],
    )
    wanted = exchange(inward, [wanted] * inner)

    chunks = call(
        functools.partial(attend, outer, inner, rows, span_lines, count, heads, step),
        [shape((heads * count, 2 * HEAD_DIM))] * inner,
        (pick, *spans, *caches, *wanted),
        [
            pltpu.VMEM((outer * span_lines, HEAD_DIM), f32),
            pltpu.VMEM((GROUP * count, 2 * HEAD_DIM), bf16),
        ],
        grant=max(8, count // 6),
    )
    chunks = exchange(inward, chunks)

    if step < HEAD_DIM:
        at = lax.rem(lax.axis_index("ctx") * step, HEAD_DIM)
        out_weight = lax.dynamic_update_slice(
            jnp.zeros((HEAD_DIM, width), out_weight.dtype), out_weight, (at, 0)
        )
    kept, *parts = call(
        functools.partial(project, inner, rows, count, heads),
        [shape((count, columns), f32)] + [shape((count, columns))] * (inner - 1),
        (*chunks, out_weight, residual_in),
        [pltpu.VMEM((count, width), f32)],
        grant=max(4, count // 12),
    )
    parts = exchange(inward, [None] + parts)[1:]
    both = [shape((count, columns), f32), shape((count, columns))]
    kept, sent = call(add_up, both, (kept, *parts))
    k = 1
    while k < outer:
        kept, sent = call(add_up, both, (kept, outward(sent, k)))
        k *= 2
    pieces = [kept] + exchange(inward, [sent] * inner)[1:]

    weights = call(
        functools.partial(route, outer, inner, rows, count, top),
        shape((count, LANES), f32),
        wanted,
        flops=10**7,
    )
    kept, sent, state = call(
        functools.partial(expert, inner, rows),
        [shape((half, width), f32), shape((half, width)), shape((rows, width), f32)],
        (expert_gate, expert_up, expert_down, norm_gain.reshape(1, width), weights, *pieces),
        [
            pltpu.VMEM((count, width), f32),
            pltpu.VMEM((count, width), bf16),
            pltpu.VMEM((count, width), f32),
        ],
        grant=max(8, count // 6),
    )
    sums = call(
        functools.partial(join, rows),
        shape((shards // 2, lines, LANES)),
        (kept, inward(sent, 1)),
        [pltpu.VMEM((half, width), f32), pltpu.VMEM((shards // 2, lines, LANES), f32)],
        grant=max(4, count // 12),
    )
    parity = [[2 * t + odd for t in range(shards // 2)] for odd in range(2)]
    back = lax.all_to_all(
        sums, "ctx", split_axis=0, concat_axis=0, tiled=True, axis_index_groups=parity
    )
    return call(
        functools.partial(combine, rows),
        shape((rows, width)),
        (state, back),
        [pltpu.VMEM((lines, LANES), f32)],
    )


def solution(mesh):
    placed = (
        P(("groups", "ctx"), None),
        P(("groups", "ctx"), None),
        P(("groups", "ctx"), None),
        P(("groups", "ctx"), None),
        P(("groups", "ctx"), None),
        P(("groups", "ctx")),
        P(("groups", "ctx"), None),
        P("ctx", None),
        P(),
        P("ctx", None, None),
        P("ctx", None, None),
        P("ctx", None, None),
        P(("groups", "ctx"), None),
        P(("groups", "ctx"), None),
    )
    return jax.shard_map(
        local, mesh=mesh, in_specs=placed, out_specs=P(("groups", "ctx"), None), check_vma=False
    )
```

profile of v0, /device:TPU:0, one launch (start us, length us, event | category | flops | bytes accessed | tf_op | source)
XLA Modules:
  0.0 58.9 jit_solution(7555261542890143340)
XLA Ops:
  0.9 0.1 shard_map.137
  1.1 3.1 %collective-permute-start = (bf16[40,128]{1,0:T(8,128)(2,1)S(1)}, bf16[40,128]{1,0:T(8,128)(2,1)S(1)}, u32[]{:S(2)}, u32[]{:S(2)}) collective-permute-start(bf16[40,128]{1,0:T(8,128)(2,1)S(1)} %get-tuple-element.34), channel_id=1, source_target_pairs={{0,4},{1,5},{2,6},{3,7},{4,0},{5,1},{6,2},{7,3},{8,12},{9,13},{10,... | collective-permute-start | bytes 30728 | tf_op jit(solution)/shard_map/ppermute | solution.py:335
  4.2 2.6 %collective-permute-start.1 = (bf16[40,128]{1,0:T(8,128)(2,1)S(1)}, bf16[40,128]{1,0:T(8,128)(2,1)S(1)}, u32[]{:S(2)}, u32[]{:S(2)}) collective-permute-start(bf16[40,128]{1,0:T(8,128)(2,1)S(1)} %get-tuple-element.35), channel_id=1, source_target_pairs={{0,8},{1,9},{2,10},{3,11},{4,12},{5,13},{6,14},{7,15},{8,0},{9,1},... | collective-permute-start | bytes 30728 | tf_op jit(solution)/shard_map/ppermute | solution.py:335
  6.8 0.9 %collective-permute-start.6 = (bf16[256,128]{1,0:T(8,128)(2,1)S(1)}, bf16[256,128]{1,0:T(8,128)(2,1)S(1)}, u32[]{:S(2)}, u32[]{:S(2)}) collective-permute-start(bf16[256,128]{1,0:T(8,128)(2,1)S(1)} %get-tuple-element.39), channel_id=1, source_target_pairs={{0,4},{1,5},{2,6},{3,7},{4,0},{5,1},{6,2},{7,3},{8,12},{9,13},{10,... | collective-permute-start | bytes 196616 | tf_op jit(solution)/shard_map/ppermute | solution.py:335
  7.8 3.5 %collective-permute-start.7 = (bf16[256,128]{1,0:T(8,128)(2,1)S(1)}, bf16[256,128]{1,0:T(8,128)(2,1)S(1)}, u32[]{:S(2)}, u32[]{:S(2)}) collective-permute-start(bf16[256,128]{1,0:T(8,128)(2,1)S(1)} %get-tuple-element.40), channel_id=1, source_target_pairs={{0,8},{1,9},{2,10},{3,11},{4,12},{5,13},{6,14},{7,15},{8,0},{9,1},... | collective-permute-start | bytes 196616 | tf_op jit(solution)/shard_map/ppermute | solution.py:335
  11.3 0.9 %collective-permute-done.2.refs_3_.refs_4_ = bf16[40,128]{1,0:T(8,128)(2,1)S(1)} collective-permute-done((bf16[40,128]{1,0:T(8,128)(2,1)S(1)}, bf16[40,128]{1,0:T(8,128)(2,1)S(1)}, u32[]{:S(2)}, u32[]{:S(2)}) %collective-permute-start.2) | collective-permute-done | bytes 10272 | tf_op jit(solution)/shard_map/ppermute | solution.py:335
  12.3 1.6 %collective-permute-start.4 = (bf16[112,128]{1,0:T(8,128)(2,1)S(1)}, bf16[112,128]{1,0:T(8,128)(2,1)S(1)}, u32[]{:S(2)}, u32[]{:S(2)}) collective-permute-start(bf16[112,128]{1,0:T(8,128)(2,1)S(1)} %shard_map.138.refs_0_.refs_9_), channel_id=1, source_target_pairs={{0,2},{1,3},{2,0},{3,1},{4,6},{5,7},{6,4},{7,5},{8,10},{9,11},{10,... | collective-permute-start | bytes 86024 | tf_op jit(solution)/shard_map/ppermute | solution.py:339
  13.9 0.9 %collective-permute-start.5 = (bf16[112,128]{1,0:T(8,128)(2,1)S(1)}, bf16[112,128]{1,0:T(8,128)(2,1)S(1)}, u32[]{:S(2)}, u32[]{:S(2)}) collective-permute-start(bf16[112,128]{1,0:T(8,128)(2,1)S(1)} %shard_map.138.refs_0_.refs_9_), channel_id=1, source_target_pairs={{0,3},{1,2},{2,1},{3,0},{4,7},{5,6},{6,5},{7,4},{8,11},{9,10},{10,... | collective-permute-start | bytes 86024 | tf_op jit(solution)/shard_map/ppermute | solution.py:339
  14.8 1.5 %collective-permute-done.4.refs_2_.refs_11_ = bf16[112,128]{1,0:T(8,128)(2,1)S(1)} collective-permute-done((bf16[112,128]{1,0:T(8,128)(2,1)S(1)}, bf16[112,128]{1,0:T(8,128)(2,1)S(1)}, u32[]{:S(2)}, u32[]{:S(2)}) %collective-permute-start.4) | collective-permute-done | bytes 28704 | tf_op jit(solution)/shard_map/ppermute | solution.py:339
  16.3 0.9 %collective-permute-done.5.refs_3_.refs_12_ = bf16[112,128]{1,0:T(8,128)(2,1)S(1)} collective-permute-done((bf16[112,128]{1,0:T(8,128)(2,1)S(1)}, bf16[112,128]{1,0:T(8,128)(2,1)S(1)}, u32[]{:S(2)}, u32[]{:S(2)}) %collective-permute-start.5) | collective-permute-done | bytes 28704 | tf_op jit(solution)/shard_map/ppermute | solution.py:339
  17.3 1.0 %shard_map.141 = (bf16[96,256]{1,0:T(8,128)(2,1)S(1)}, bf16[96,256]{1,0:T(8,128)(2,1)S(1)}, bf16[96,256]{1,0:T(8,128)(2,1)S(1)}, bf16[96,256]{1,0:T(8,128)(2,1)S(1)}) custom-call(bf16[384,384]{1,0:T(8,128)(2,1)S(1)} %get-tuple-element.37.refs_0_, bf16[40,128]{1,0:T(8,128)(2,1)S(1)} %get-tuple-element.33.refs_0_.refs_1_, ...), custom_call_target="tpu_custom_call" | custom-call | flops 1000000000 | bytes 1000000 | tf_op jit(solution)/shard_map/pallas_call | solution.py:30
  18.3 1.6 %collective-permute-start.10 = (bf16[96,256]{1,0:T(8,128)(2,1)S(1)}, bf16[96,256]{1,0:T(8,128)(2,1)S(1)}, u32[]{:S(2)}, u32[]{:S(2)}) collective-permute-start(bf16[96,256]{1,0:T(8,128)(2,1)S(1)} %get-tuple-element.44), channel_id=1, source_target_pairs={{0,2},{1,3},{2,0},{3,1},{4,6},{5,7},{6,4},{7,5},{8,10},{9,11},{10,... | collective-permute-start | bytes 147464 | tf_op jit(solution)/shard_map/ppermute | solution.py:339
  19.9 0.6 %collective-permute-start.9 = (bf16[96,256]{1,0:T(8,128)(2,1)S(1)}, bf16[96,256]{1,0:T(8,128)(2,1)S(1)}, u32[]{:S(2)}, u32[]{:S(2)}) collective-permute-start(bf16[96,256]{1,0:T(8,128)(2,1)S(1)} %get-tuple-element.43), channel_id=1, source_target_pairs={{0,1},{1,0},{2,3},{3,2},{4,5},{5,4},{6,7},{7,6},{8,9},{9,8},{10,11... | collective-permute-start | bytes 147464 | tf_op jit(solution)/shard_map/ppermute | solution.py:339
  20.5 1.9 %collective-permute-done.10.refs_2_ = bf16[96,256]{1,0:T(8,128)(2,1)S(1)} collective-permute-done((bf16[96,256]{1,0:T(8,128)(2,1)S(1)}, bf16[96,256]{1,0:T(8,128)(2,1)S(1)}, u32[]{:S(2)}, u32[]{:S(2)}) %collective-permute-start.10) | collective-permute-done | bytes 49184 | tf_op jit(solution)/shard_map/ppermute | solution.py:339
  22.5 1.3 %collective-permute-done.11.refs_3_ = bf16[96,256]{1,0:T(8,128)(2,1)S(1)} collective-permute-done((bf16[96,256]{1,0:T(8,128)(2,1)S(1)}, bf16[96,256]{1,0:T(8,128)(2,1)S(1)}, u32[]{:S(2)}, u32[]{:S(2)}) %collective-permute-start.11) | collective-permute-done | bytes 49184 | tf_op jit(solution)/shard_map/ppermute | solution.py:339
  23.8 0.6 %shard_map.142 = (f32[48,512]{1,0:T(8,128)S(1)}, bf16[48,512]{1,0:T(8,128)(2,1)S(1)}, bf16[48,512]{1,0:T(8,128)(2,1)S(1)}, bf16[48,512]{1,0:T(8,128)(2,1)S(1)}) custom-call(bf16[96,256]{1,0:T(8,128)(2,1)S(1)} %get-tuple-element.42.refs_0_, bf16[96,256]{1,0:T(8,128)(2,1)S(1)} %collective-permute-done.9.refs_1_, ...), custom_call_target="tpu_custom_call" | custom-call | flops 1000000000 | bytes 1000000 | tf_op jit(solution)/shard_map/pallas_call | solution.py:30
  24.5 1.0 %collective-permute-start.13 = (bf16[48,512]{1,0:T(8,128)(2,1)S(1)}, bf16[48,512]{1,0:T(8,128)(2,1)S(1)}, u32[]{:S(2)}, u32[]{:S(2)}) collective-permute-start(bf16[48,512]{1,0:T(8,128)(2,1)S(1)} %get-tuple-element.48), channel_id=1, source_target_pairs={{0,2},{1,3},{2,0},{3,1},{4,6},{5,7},{6,4},{7,5},{8,10},{9,11},{10,... | collective-permute-start | bytes 147464 | tf_op jit(solution)/shard_map/ppermute | solution.py:339
  25.5 0.9 %collective-permute-start.14 = (bf16[48,512]{1,0:T(8,128)(2,1)S(1)}, bf16[48,512]{1,0:T(8,128)(2,1)S(1)}, u32[]{:S(2)}, u32[]{:S(2)}) collective-permute-start(bf16[48,512]{1,0:T(8,128)(2,1)S(1)} %get-tuple-element.49), channel_id=1, source_target_pairs={{0,3},{1,2},{2,1},{3,0},{4,7},{5,6},{6,5},{7,4},{8,11},{9,10},{10,... | collective-permute-start | bytes 147464 | tf_op jit(solution)/shard_map/ppermute | solution.py:339
  26.4 2.5 %collective-permute-done.13.refs_1_ = bf16[48,512]{1,0:T(8,128)(2,1)S(1)} collective-permute-done((bf16[48,512]{1,0:T(8,128)(2,1)S(1)}, bf16[48,512]{1,0:T(8,128)(2,1)S(1)}, u32[]{:S(2)}, u32[]{:S(2)}) %collective-permute-start.13) | collective-permute-done | bytes 49184 | tf_op jit(solution)/shard_map/ppermute | solution.py:339
  28.9 0.7 %collective-permute-done.14.refs_2_ = bf16[48,512]{1,0:T(8,128)(2,1)S(1)} collective-permute-done((bf16[48,512]{1,0:T(8,128)(2,1)S(1)}, bf16[48,512]{1,0:T(8,128)(2,1)S(1)}, u32[]{:S(2)}, u32[]{:S(2)}) %collective-permute-start.14) | collective-permute-done | bytes 49184 | tf_op jit(solution)/shard_map/ppermute | solution.py:339
  29.7 4.1 %collective-permute-done.15.refs_0_ = bf16[48,512]{1,0:T(8,128)(2,1)S(1)} collective-permute-done((bf16[48,512]{1,0:T(8,128)(2,1)S(1)}, bf16[48,512]{1,0:T(8,128)(2,1)S(1)}, u32[]{:S(2)}, u32[]{:S(2)}) %collective-permute-start.15) | collective-permute-done | bytes 49184 | tf_op jit(solution)/shard_map/ppermute | solution.py:335
  33.8 1.1 %collective-permute-start.16 = (bf16[48,512]{1,0:T(8,128)(2,1)S(1)}, bf16[48,512]{1,0:T(8,128)(2,1)S(1)}, u32[]{:S(2)}, u32[]{:S(2)}) collective-permute-start(bf16[48,512]{1,0:T(8,128)(2,1)S(1)} %get-tuple-element.53), channel_id=1, source_target_pairs={{0,8},{1,9},{2,10},{3,11},{4,12},{5,13},{6,14},{7,15},{8,0},{9,1},... | collective-permute-start | bytes 147464 | tf_op jit(solution)/shard_map/ppermute | solution.py:335
  34.9 4.1 %collective-permute-done.16.refs_0_ = bf16[48,512]{1,0:T(8,128)(2,1)S(1)} collective-permute-done((bf16[48,512]{1,0:T(8,128)(2,1)S(1)}, bf16[48,512]{1,0:T(8,128)(2,1)S(1)}, u32[]{:S(2)}, u32[]{:S(2)}) %collective-permute-start.16) | collective-permute-done | bytes 49184 | tf_op jit(solution)/shard_map/ppermute | solution.py:335
  39.0 1.0 %collective-permute-start.18 = (bf16[48,512]{1,0:T(8,128)(2,1)S(1)}, bf16[48,512]{1,0:T(8,128)(2,1)S(1)}, u32[]{:S(2)}, u32[]{:S(2)}) collective-permute-start(bf16[48,512]{1,0:T(8,128)(2,1)S(1)} %get-tuple-element.55), channel_id=1, source_target_pairs={{0,2},{1,3},{2,0},{3,1},{4,6},{5,7},{6,4},{7,5},{8,10},{9,11},{10,... | collective-permute-start | bytes 147464 | tf_op jit(solution)/shard_map/ppermute | solution.py:339
  40.0 0.9 %collective-permute-start.19 = (bf16[48,512]{1,0:T(8,128)(2,1)S(1)}, bf16[48,512]{1,0:T(8,128)(2,1)S(1)}, u32[]{:S(2)}, u32[]{:S(2)}) collective-permute-start(bf16[48,512]{1,0:T(8,128)(2,1)S(1)} %get-tuple-element.55), channel_id=1, source_target_pairs={{0,3},{1,2},{2,1},{3,0},{4,7},{5,6},{6,5},{7,4},{8,11},{9,10},{10,... | collective-permute-start | bytes 147464 | tf_op jit(solution)/shard_map/ppermute | solution.py:339
  41.0 2.4 %collective-permute-done.18.refs_2_ = bf16[48,512]{1,0:T(8,128)(2,1)S(1)} collective-permute-done((bf16[48,512]{1,0:T(8,128)(2,1)S(1)}, bf16[48,512]{1,0:T(8,128)(2,1)S(1)}, u32[]{:S(2)}, u32[]{:S(2)}) %collective-permute-start.18) | collective-permute-done | bytes 49184 | tf_op jit(solution)/shard_map/ppermute | solution.py:339
  43.4 0.7 %collective-permute-done.19.refs_3_ = bf16[48,512]{1,0:T(8,128)(2,1)S(1)} collective-permute-done((bf16[48,512]{1,0:T(8,128)(2,1)S(1)}, bf16[48,512]{1,0:T(8,128)(2,1)S(1)}, u32[]{:S(2)}, u32[]{:S(2)}) %collective-permute-start.19) | collective-permute-done | bytes 49184 | tf_op jit(solution)/shard_map/ppermute | solution.py:339
  44.0 2.0 %shard_map.146 = (f32[24,2048]{1,0:T(8,128)S(1)}, bf16[24,2048]{1,0:T(8,128)(2,1)S(1)}, f32[3,2048]{1,0:T(4,128)S(1)}) custom-call(bf16[1,2048,768]{2,1,0:T(8,128)(2,1)S(1)} %copy-done, bf16[1,2048,768]{2,1,0:T(8,128)(2,1)S(1)} %copy-done.1, bf16[1,768,2048]{2,1,0:T(8,128)(2,1)S(1)} %copy-done.2, bf16[1,2048]{1,0:T(2,128)(2,1)S(1)} %reshape.3.gain, ...), custom_call_target="tpu_custom_call" | custom-call | flops 1000000000 | bytes 1000000 | tf_op jit(solution)/shard_map/pallas_call | solution.py:30
  46.0 0.2 collective-permute-start.20
  46.2 1.2 %collective-permute-done.20.other = bf16[24,2048]{1,0:T(8,128)(2,1)S(1)} collective-permute-done((bf16[24,2048]{1,0:T(8,128)(2,1)S(1)}, bf16[24,2048]{1,0:T(8,128)(2,1)S(1)}, u32[]{:S(2)}, u32[]{:S(2)}) %collective-permute-start.20) | collective-permute-done | bytes 98336 | tf_op jit(solution)/shard_map/ppermute | solution.py:339
  47.5 10.8 %all_to_all.5.back = bf16[8,48,128]{2,1,0:T(8,128)(2,1)S(1)} all-to-all(bf16[8,48,128]{2,1,0:T(8,128)(2,1)S(1)} %shard_map.147), channel_id=1, replica_groups={{0,2,4,6,8,10,12,14},{1,3,5,7,9,11,13,15},{16,18,20,22,24,26,28,30},{17..., dimensions={0} | all-to-all | bytes 196608 | tf_op jit(solution)/shard_map/all_to_all | solution.py:435
  58.3 0.6 %shard_map.148 = bf16[3,2048]{1,0:T(4,128)(2,1)} custom-call(f32[3,2048]{1,0:T(4,128)S(1)} %get-tuple-element.56.state, bf16[8,48,128]{2,1,0:T(8,128)(2,1)S(1)} %all_to_all.5.back), custom_call_target="tpu_custom_call" | custom-call | flops 1000000000 | bytes 1000000 | tf_op jit(solution)/shard_map/pallas_call | solution.py:30
  (51 shorter events, 0.9 us)
Async XLA Ops:
  0.0 0.9 %copy-start.9 = (bf16[3,512]{1,0:T(4,128)(2,1)S(1)}, bf16[3,512]{1,0:T(4,128)(2,1)}, u32[]{:S(2)}) copy-start(bf16[3,512]{1,0:T(4,128)(2,1)} %new_values.1) | copy-start | bytes 9220
  0.0 0.9 %copy-start.10 = (s32[3,8]{1,0:T(4,128)S(1)}, s32[3,8]{1,0:T(4,128)}, u32[]{:S(2)}) copy-start(s32[3,8]{1,0:T(4,128)} %ids.1) | copy-start | bytes 292
  0.0 0.9 %copy-start.11 = (f32[3,8]{1,0:T(4,128)S(1)}, f32[3,8]{1,0:T(4,128)}, u32[]{:S(2)}) copy-start(f32[3,8]{1,0:T(4,128)} %weights.1) | copy-start | bytes 292
  0.0 6.7 %copy-start.4 = (bf16[128,512]{1,0:T(8,128)(2,1)S(1)}, bf16[128,512]{1,0:T(8,128)(2,1)}, u32[]{:S(2)}) copy-start(bf16[128,512]{1,0:T(8,128)(2,1)} %keys.1) | copy-start | bytes 393220
  0.0 6.7 %copy-start.5 = (bf16[128,512]{1,0:T(8,128)(2,1)S(1)}, bf16[128,512]{1,0:T(8,128)(2,1)}, u32[]{:S(2)}) copy-start(bf16[128,512]{1,0:T(8,128)(2,1)} %values.1) | copy-start | bytes 393220
  1.1 10.2 %collective-permute-start = (bf16[40,128]{1,0:T(8,128)(2,1)S(1)}, bf16[40,128]{1,0:T(8,128)(2,1)S(1)}, u32[]{:S(2)}, u32[]{:S(2)}) collective-permute-start(bf16[40,128]{1,0:T(8,128)(2,1)S(1)} %get-tuple-element.34), channel_id=1, source_target_pairs={{0,4},{1,5},{2,6},{3,7},{4,0},{5,1},{6,2},{7,3},{8,12},{9,13},{10,... | collective-permute-start | bytes 30728 | tf_op jit(solution)/shard_map/ppermute | solution.py:335
  4.2 7.1 %collective-permute-start.1 = (bf16[40,128]{1,0:T(8,128)(2,1)S(1)}, bf16[40,128]{1,0:T(8,128)(2,1)S(1)}, u32[]{:S(2)}, u32[]{:S(2)}) collective-permute-start(bf16[40,128]{1,0:T(8,128)(2,1)S(1)} %get-tuple-element.35), channel_id=1, source_target_pairs={{0,8},{1,9},{2,10},{3,11},{4,12},{5,13},{6,14},{7,15},{8,0},{9,1},... | collective-permute-start | bytes 30728 | tf_op jit(solution)/shard_map/ppermute | solution.py:335
  6.8 5.5 %collective-permute-start.2 = (bf16[40,128]{1,0:T(8,128)(2,1)S(1)}, bf16[40,128]{1,0:T(8,128)(2,1)S(1)}, u32[]{:S(2)}, u32[]{:S(2)}) collective-permute-start(bf16[40,128]{1,0:T(8,128)(2,1)S(1)} %get-tuple-element.36), channel_id=1, source_target_pairs={{0,12},{1,13},{2,14},{3,15},{4,8},{5,9},{6,10},{7,11},{8,4},{9,5},... | collective-permute-start | bytes 30728 | tf_op jit(solution)/shard_map/ppermute | solution.py:335
  6.8 10.4 %collective-permute-start.6 = (bf16[256,128]{1,0:T(8,128)(2,1)S(1)}, bf16[256,128]{1,0:T(8,128)(2,1)S(1)}, u32[]{:S(2)}, u32[]{:S(2)}) collective-permute-start(bf16[256,128]{1,0:T(8,128)(2,1)S(1)} %get-tuple-element.39), channel_id=1, source_target_pairs={{0,4},{1,5},{2,6},{3,7},{4,0},{5,1},{6,2},{7,3},{8,12},{9,13},{10,... | collective-permute-start | bytes 196616 | tf_op jit(solution)/shard_map/ppermute | solution.py:335
  7.8 9.4 %collective-permute-start.7 = (bf16[256,128]{1,0:T(8,128)(2,1)S(1)}, bf16[256,128]{1,0:T(8,128)(2,1)S(1)}, u32[]{:S(2)}, u32[]{:S(2)}) collective-permute-start(bf16[256,128]{1,0:T(8,128)(2,1)S(1)} %get-tuple-element.40), channel_id=1, source_target_pairs={{0,8},{1,9},{2,10},{3,11},{4,12},{5,13},{6,14},{7,15},{8,0},{9,1},... | collective-permute-start | bytes 196616 | tf_op jit(solution)/shard_map/ppermute | solution.py:335
  11.3 6.1 %collective-permute-start.8 = (bf16[256,128]{1,0:T(8,128)(2,1)S(1)}, bf16[256,128]{1,0:T(8,128)(2,1)S(1)}, u32[]{:S(2)}, u32[]{:S(2)}) collective-permute-start(bf16[256,128]{1,0:T(8,128)(2,1)S(1)} %get-tuple-element.41), channel_id=1, source_target_pairs={{0,12},{1,13},{2,14},{3,15},{4,8},{5,9},{6,10},{7,11},{8,4},{9,5},... | collective-permute-start | bytes 196616 | tf_op jit(solution)/shard_map/ppermute | solution.py:335
  12.2 11.6 %copy-start.3 = (bf16[256,2048]{1,0:T(8,128)(2,1)S(1)}, bf16[256,2048]{1,0:T(8,128)(2,1)}, u32[]{:S(2)}) copy-start(bf16[256,2048]{1,0:T(8,128)(2,1)} %refs_4_.1) | copy-start | bytes 3145732
  12.2 11.6 %copy-start.7 = (bf16[3,2048]{1,0:T(4,128)(2,1)S(1)}, bf16[3,2048]{1,0:T(4,128)(2,1)}, u32[]{:S(2)}) copy-start(bf16[3,2048]{1,0:T(4,128)(2,1)} %refs_5_.1) | copy-start | bytes 36868
  12.2 1.7 %collective-permute-start.3 = (bf16[112,128]{1,0:T(8,128)(2,1)S(1)}, bf16[112,128]{1,0:T(8,128)(2,1)S(1)}, u32[]{:S(2)}, u32[]{:S(2)}) collective-permute-start(bf16[112,128]{1,0:T(8,128)(2,1)S(1)} %shard_map.138.refs_0_.refs_9_), channel_id=1, source_target_pairs={{0,1},{1,0},{2,3},{3,2},{4,5},{5,4},{6,7},{7,6},{8,9},{9,8},{10,11... | collective-permute-start | bytes 86024 | tf_op jit(solution)/shard_map/ppermute | solution.py:339
  12.3 3.9 %collective-permute-start.4 = (bf16[112,128]{1,0:T(8,128)(2,1)S(1)}, bf16[112,128]{1,0:T(8,128)(2,1)S(1)}, u32[]{:S(2)}, u32[]{:S(2)}) collective-permute-start(bf16[112,128]{1,0:T(8,128)(2,1)S(1)} %shard_map.138.refs_0_.refs_9_), channel_id=1, source_target_pairs={{0,2},{1,3},{2,0},{3,1},{4,6},{5,7},{6,4},{7,5},{8,10},{9,11},{10,... | collective-permute-start | bytes 86024 | tf_op jit(solution)/shard_map/ppermute | solution.py:339
  13.9 3.3 %collective-permute-start.5 = (bf16[112,128]{1,0:T(8,128)(2,1)S(1)}, bf16[112,128]{1,0:T(8,128)(2,1)S(1)}, u32[]{:S(2)}, u32[]{:S(2)}) collective-permute-start(bf16[112,128]{1,0:T(8,128)(2,1)S(1)} %shard_map.138.refs_0_.refs_9_), channel_id=1, source_target_pairs={{0,3},{1,2},{2,1},{3,0},{4,7},{5,6},{6,5},{7,4},{8,11},{9,10},{10,... | collective-permute-start | bytes 86024 | tf_op jit(solution)/shard_map/ppermute | solution.py:339
  18.3 4.2 %collective-permute-start.10 = (bf16[96,256]{1,0:T(8,128)(2,1)S(1)}, bf16[96,256]{1,0:T(8,128)(2,1)S(1)}, u32[]{:S(2)}, u32[]{:S(2)}) collective-permute-start(bf16[96,256]{1,0:T(8,128)(2,1)S(1)} %get-tuple-element.44), channel_id=1, source_target_pairs={{0,2},{1,3},{2,0},{3,1},{4,6},{5,7},{6,4},{7,5},{8,10},{9,11},{10,... | collective-permute-start | bytes 147464 | tf_op jit(solution)/shard_map/ppermute | solution.py:339
  19.9 3.9 %collective-permute-start.11 = (bf16[96,256]{1,0:T(8,128)(2,1)S(1)}, bf16[96,256]{1,0:T(8,128)(2,1)S(1)}, u32[]{:S(2)}, u32[]{:S(2)}) collective-permute-start(bf16[96,256]{1,0:T(8,128)(2,1)S(1)} %get-tuple-element.45), channel_id=1, source_target_pairs={{0,3},{1,2},{2,1},{3,0},{4,7},{5,6},{6,5},{7,4},{8,11},{9,10},{10,... | collective-permute-start | bytes 147464 | tf_op jit(solution)/shard_map/ppermute | solution.py:339
  19.9 3.9 %collective-permute-start.9 = (bf16[96,256]{1,0:T(8,128)(2,1)S(1)}, bf16[96,256]{1,0:T(8,128)(2,1)S(1)}, u32[]{:S(2)}, u32[]{:S(2)}) collective-permute-start(bf16[96,256]{1,0:T(8,128)(2,1)S(1)} %get-tuple-element.43), channel_id=1, source_target_pairs={{0,1},{1,0},{2,3},{3,2},{4,5},{5,4},{6,7},{7,6},{8,9},{9,8},{10,11... | collective-permute-start | bytes 147464 | tf_op jit(solution)/shard_map/ppermute | solution.py:339
  24.4 1.9 %collective-permute-start.12 = (bf16[48,512]{1,0:T(8,128)(2,1)S(1)}, bf16[48,512]{1,0:T(8,128)(2,1)S(1)}, u32[]{:S(2)}, u32[]{:S(2)}) collective-permute-start(bf16[48,512]{1,0:T(8,128)(2,1)S(1)} %get-tuple-element.47), channel_id=1, source_target_pairs={{0,1},{1,0},{2,3},{3,2},{4,5},{5,4},{6,7},{7,6},{8,9},{9,8},{10,11... | collective-permute-start | bytes 147464 | tf_op jit(solution)/shard_map/ppermute | solution.py:339
  24.5 4.3 %collective-permute-start.13 = (bf16[48,512]{1,0:T(8,128)(2,1)S(1)}, bf16[48,512]{1,0:T(8,128)(2,1)S(1)}, u32[]{:S(2)}, u32[]{:S(2)}) collective-permute-start(bf16[48,512]{1,0:T(8,128)(2,1)S(1)} %get-tuple-element.48), channel_id=1, source_target_pairs={{0,2},{1,3},{2,0},{3,1},{4,6},{5,7},{6,4},{7,5},{8,10},{9,11},{10,... | collective-permute-start | bytes 147464 | tf_op jit(solution)/shard_map/ppermute | solution.py:339
  25.5 4.0 %collective-permute-start.14 = (bf16[48,512]{1,0:T(8,128)(2,1)S(1)}, bf16[48,512]{1,0:T(8,128)(2,1)S(1)}, u32[]{:S(2)}, u32[]{:S(2)}) collective-permute-start(bf16[48,512]{1,0:T(8,128)(2,1)S(1)} %get-tuple-element.49), channel_id=1, source_target_pairs={{0,3},{1,2},{2,1},{3,0},{4,7},{5,6},{6,5},{7,4},{8,11},{9,10},{10,... | collective-permute-start | bytes 147464 | tf_op jit(solution)/shard_map/ppermute | solution.py:339
  29.5 14.5 %copy-start.2 = (bf16[1,768,2048]{2,1,0:T(8,128)(2,1)S(1)}, bf16[1,768,2048]{2,1,0:T(8,128)(2,1)}, u32[]{:S(2)}) copy-start(bf16[1,768,2048]{2,1,0:T(8,128)(2,1)} %down.1) | copy-start | bytes 9437188
  29.6 4.2 %collective-permute-start.15 = (bf16[48,512]{1,0:T(8,128)(2,1)S(1)}, bf16[48,512]{1,0:T(8,128)(2,1)S(1)}, u32[]{:S(2)}, u32[]{:S(2)}) collective-permute-start(bf16[48,512]{1,0:T(8,128)(2,1)S(1)} %get-tuple-element.51), channel_id=1, source_target_pairs={{0,4},{1,5},{2,6},{3,7},{4,0},{5,1},{6,2},{7,3},{8,12},{9,13},{10,... | collective-permute-start | bytes 147464 | tf_op jit(solution)/shard_map/ppermute | solution.py:335
  33.7 7.1 %copy-start.12 = (bf16[2048]{0:T(1024)(128)(2,1)S(1)}, bf16[2048]{0:T(1024)(128)(2,1)}, u32[]{:S(2)}) copy-start(bf16[2048]{0:T(1024)(128)(2,1)} %param.22) | copy-start | bytes 12292
  33.7 10.3 %copy-start = (bf16[1,2048,768]{2,1,0:T(8,128)(2,1)S(1)}, bf16[1,2048,768]{2,1,0:T(8,128)(2,1)}, u32[]{:S(2)}) copy-start(bf16[1,2048,768]{2,1,0:T(8,128)(2,1)} %gate.1) | copy-start | bytes 9437188
  33.7 10.3 %copy-start.1 = (bf16[1,2048,768]{2,1,0:T(8,128)(2,1)S(1)}, bf16[1,2048,768]{2,1,0:T(8,128)(2,1)}, u32[]{:S(2)}) copy-start(bf16[1,2048,768]{2,1,0:T(8,128)(2,1)} %up.1) | copy-start | bytes 9437188
  33.8 5.2 %collective-permute-start.16 = (bf16[48,512]{1,0:T(8,128)(2,1)S(1)}, bf16[48,512]{1,0:T(8,128)(2,1)S(1)}, u32[]{:S(2)}, u32[]{:S(2)}) collective-permute-start(bf16[48,512]{1,0:T(8,128)(2,1)S(1)} %get-tuple-element.53), channel_id=1, source_target_pairs={{0,8},{1,9},{2,10},{3,11},{4,12},{5,13},{6,14},{7,15},{8,0},{9,1},... | collective-permute-start | bytes 147464 | tf_op jit(solution)/shard_map/ppermute | solution.py:335
  38.9 2.1 %collective-permute-start.17 = (bf16[48,512]{1,0:T(8,128)(2,1)S(1)}, bf16[48,512]{1,0:T(8,128)(2,1)S(1)}, u32[]{:S(2)}, u32[]{:S(2)}) collective-permute-start(bf16[48,512]{1,0:T(8,128)(2,1)S(1)} %get-tuple-element.55), channel_id=1, source_target_pairs={{0,1},{1,0},{2,3},{3,2},{4,5},{5,4},{6,7},{7,6},{8,9},{9,8},{10,11... | collective-permute-start | bytes 147464 | tf_op jit(solution)/shard_map/ppermute | solution.py:339
  39.0 4.3 %collective-permute-start.18 = (bf16[48,512]{1,0:T(8,128)(2,1)S(1)}, bf16[48,512]{1,0:T(8,128)(2,1)S(1)}, u32[]{:S(2)}, u32[]{:S(2)}) collective-permute-start(bf16[48,512]{1,0:T(8,128)(2,1)S(1)} %get-tuple-element.55), channel_id=1, source_target_pairs={{0,2},{1,3},{2,0},{3,1},{4,6},{5,7},{6,4},{7,5},{8,10},{9,11},{10,... | collective-permute-start | bytes 147464 | tf_op jit(solution)/shard_map/ppermute | solution.py:339
  40.0 4.0 %collective-permute-start.19 = (bf16[48,512]{1,0:T(8,128)(2,1)S(1)}, bf16[48,512]{1,0:T(8,128)(2,1)S(1)}, u32[]{:S(2)}, u32[]{:S(2)}) collective-permute-start(bf16[48,512]{1,0:T(8,128)(2,1)S(1)} %get-tuple-element.55), channel_id=1, source_target_pairs={{0,3},{1,2},{2,1},{3,0},{4,7},{5,6},{6,5},{7,4},{8,11},{9,10},{10,... | collective-permute-start | bytes 147464 | tf_op jit(solution)/shard_map/ppermute | solution.py:339
  46.0 1.4 %collective-permute-start.20 = (bf16[24,2048]{1,0:T(8,128)(2,1)S(1)}, bf16[24,2048]{1,0:T(8,128)(2,1)S(1)}, u32[]{:S(2)}, u32[]{:S(2)}) collective-permute-start(bf16[24,2048]{1,0:T(8,128)(2,1)S(1)} %get-tuple-element.58), channel_id=1, source_target_pairs={{0,1},{1,0},{2,3},{3,2},{4,5},{5,4},{6,7},{7,6},{8,9},{9,8},{10,11... | collective-permute-start | bytes 294920 | tf_op jit(solution)/shard_map/ppermute | solution.py:339
  (2 other events, 1.7 us)
where the time goes:
time: 59.1 us; the launch traced here: 58.9 us
  waiting for transfers between devices  22.3 us (38%)
  starting transfers between devices  20.1 us (34%)
  blocking collectives  10.8 us (18%)
  Pallas kernels  4.75 us (8%)
  between operations  0.93 us (2%)
    ppermute x13, waiting for transfers between devices, inward(): return lax.ppermute(x, 'ctx', pairs)  13.1 us
    ppermute x8, starting transfers between devices, outward(): return lax.ppermute(x, 'ctx', pairs)  11.3 us
    all_to_all x1, blocking collectives, local(): lax.all_to_all(sums, 'ctx', split_axis=0, concat_axis=0, tiled=True, axis...  10.8 us
    ppermute x8, waiting for transfers between devices, outward(): return lax.ppermute(x, 'ctx', pairs)  9.19 us
    ppermute x13, starting transfers between devices, inward(): return lax.ppermute(x, 'ctx', pairs)  8.76 us
    pallas_call x13, Pallas kernels, call(): pl.pallas_call(body, out_shape=outs, in_specs=[VMEM] * len(operands), out...  4.75 us
  transfers between devices with their start and end apart: 21, of which 13 were waited for; matrix products, arithmetic and copies ran while one was open for 0% of the time, Pallas kernels for 0%

commit v1 on v0

--- a/solution.py
+++ b/solution.py
@@ -51,6 +51,17 @@
 
 def place(shard, half, rows):
     return jnp.bitwise_and(shard, 1) * half + jnp.right_shift(shard, 1) * rows
+
+
+def stat_lines(lines):
+    starts = range(0, lines, LANES)
+    return [(s, min(LANES, lines - s), lines + 16 * i) for i, s in enumerate(starts)]
+
+
+def selection():
+    line = lax.broadcasted_iota(jnp.int32, (16, LANES), 0)
+    lane = lax.broadcasted_iota(jnp.int32, (16, LANES), 1)
+    return jnp.where(line == lane, 1.0, 0.0).astype(bf16)
 
 
 def aligned(index, size):
@@ -195,19 +206,41 @@
     parts[:, HEAD_DIM:] = stats.astype(bf16)
     for k in range(inner):
         first = jnp.right_shift(jnp.bitwise_xor(b, k) * step, HEAD_DIM.bit_length() - 1)
-        outs[k][...] = parts[pl.ds(pl.multiple_of(first * count, 16), heads * count)]
+        first, lines = pl.multiple_of(first * count, 16), heads * count
+        outs[k][0:lines] = parts[pl.ds(first, lines), 0:HEAD_DIM]
+        outs[k][lines:] = jnp.zeros((outs[k].shape[0] - lines, LANES), bf16)
+        for start, size, at in stat_lines(lines):
+            block = parts[pl.ds(pl.multiple_of(first + start, 16), size), HEAD_DIM:]
+            outs[k][at : at + 16, 0:size] = lax.dot_general(
+                selection(), block, (((1,), (1,)), ((), ())), preferred_element_type=f32
+            ).astype(bf16)
 
 
 def project(inner, rows, count, heads, *refs):
     chunks, (weight, residual), refs = refs[:inner], refs[inner : inner + 2], refs[inner + 2 :]
     own, outs, total = refs[0], refs[1:inner], refs[inner]
     _, b = coordinates(inner)
-    stats = [chunk[:, HEAD_DIM:].astype(f32) for chunk in chunks]
+    lines = heads * count
+    stats = [
+        jnp.concatenate(
+            [
+                lax.dot_general(
+                    chunk[at : at + 16, 0:size],
+                    selection(),
+                    (((0,), (0,)), ((), ())),
+                    preferred_element_type=f32,
+                )
+                for _, size, at in stat_lines(lines)
+            ],
+            0,
+        )
+        for chunk in chunks
+    ]
     largest = functools.reduce(jnp.maximum, [s[:, 0:1] for s in stats])
     scales = [jnp.exp(s[:, 0:1] - largest) for s in stats]
     denominator = sum(w * (s[:, 1:2] + s[:, 2:3]) for w, s in zip(scales, stats))
     joined = sum(
-        chunk[:, 0:HEAD_DIM].astype(f32) * (w / denominator)
+        chunk[0:lines].astype(f32) * (w / denominator)
         for w, chunk in zip(scales, chunks)
     ).astype(bf16)
     total[...] = sum(
@@ -256,24 +289,42 @@
                 out[pl.ds(place(shard, count // 2, rows) + r, 1)] = share[k : k + 1]
 
 
-def expert(inner, rows, gate, up, down, gain, weights, *refs):
-    pieces, (kept, sent, mine, state, normed, held) = refs[:inner], refs[inner:]
+def begin(inner, gate, up, gain, *refs):
+    pieces, (gated, lifted, squares) = refs[:-3], refs[-3:]
+    _, b = coordinates(inner)
+    columns = pieces[0].shape[1]
+    total, sums = jnp.zeros(squares.shape, f32), [0.0, 0.0]
+    for k, piece in enumerate(pieces):
+        lanes = aligned(jnp.bitwise_xor(b, k), columns)
+        value = piece[...].astype(f32)
+        total = total + jnp.sum(value * value, axis=1, keepdims=True)
+        x = (value * gain[:, lanes].astype(f32)).astype(bf16)
+        for i, weight in enumerate((gate, up)):
+            sums[i] = sums[i] + jnp.dot(x, weight[0, lanes], preferred_element_type=f32)
+    gated[...], lifted[...] = sums
+    squares[...] = total
+
+
+def expert(inner, early, rows, gate, up, down, gain, weights, begun_gate, begun_up, begun, *refs):
+    pieces, (kept, sent, mine, state, held) = refs[:inner], refs[inner:]
     _, b = coordinates(inner)
     columns = pieces[0].shape[1]
     half = kept.shape[0]
-    values = [piece[...].astype(f32) for piece in pieces]
-    squares = sum(jnp.sum(v * v, axis=1, keepdims=True) for v in values)
+    squares, gated, lifted = begun[:, 0:1], begun_gate[...], begun_up[...]
+    for k, piece in enumerate(pieces):
+        lanes = aligned(jnp.bitwise_xor(b, k), columns)
+        value = piece[...].astype(f32)
+        state[:, lanes] = value
+        if k >= early:
+            squares = squares + jnp.sum(value * value, axis=1, keepdims=True)
+            x = (value * gain[:, lanes].astype(f32)).astype(bf16)
+            gated = gated + jnp.dot(x, gate[0, lanes], preferred_element_type=f32)
+            lifted = lifted + jnp.dot(x, up[0, lanes], preferred_element_type=f32)
     scale = lax.rsqrt(squares * (1.0 / (inner * columns)) + epsilon)
-    for k, value in enumerate(values):
-        lanes = aligned(jnp.bitwise_xor(b, k), columns)
-        state[:, lanes] = value
-        normed[:, lanes] = (value * scale * gain[:, lanes].astype(f32)).astype(bf16)
+    gated, lifted = gated * scale, lifted * scale
     start = place(lax.axis_index("ctx"), half, rows)
     for r in range(rows):
         mine[r : r + 1] = state[pl.ds(start + r, 1)]
-    x = normed[...]
-    gated = jnp.dot(x, gate[0], preferred_element_type=f32)
-    lifted = jnp.dot(x, up[0], preferred_element_type=f32)
     active = (gated / (1.0 + jnp.exp(-gated)) * lifted).astype(bf16)
     held[...] = jnp.dot(active, down[0], preferred_element_type=f32) * weights[:, 0:1]
     odd = jnp.bitwise_and(b, 1)
@@ -376,7 +427,7 @@
 
     chunks = call(
         functools.partial(attend, outer, inner, rows, span_lines, count, heads, step),
-        [shape((heads * count, 2 * HEAD_DIM))] * inner,
+        [shape((stat_lines(heads * count)[-1][2] + 16, HEAD_DIM))] * inner,
         (pick, *spans, *caches, *wanted),
         [
             pltpu.VMEM((outer * span_lines, HEAD_DIM), f32),
@@ -413,15 +464,19 @@
         wanted,
         flops=10**7,
     )
+    early = min(2, inner)
+    hidden = shape((count, expert_gate.shape[2]), f32)
+    gain = norm_gain.reshape(1, width)
+    begun = call(
+        functools.partial(begin, inner),
+        [hidden, hidden, shape((count, LANES), f32)],
+        (expert_gate, expert_up, gain, *pieces[:early]),
+    )
     kept, sent, state = call(
-        functools.partial(expert, inner, rows),
+        functools.partial(expert, inner, early, rows),
         [shape((half, width), f32), shape((half, width)), shape((rows, width), f32)],
-        (expert_gate, expert_up, expert_down, norm_gain.reshape(1, width), weights, *pieces),
-        [
-            pltpu.VMEM((count, width), f32),
-            pltpu.VMEM((count, width), bf16),
-            pltpu.VMEM((count, width), f32),
-        ],
+        (expert_gate, expert_up, expert_down, gain, weights, *begun, *pieces),
+        [pltpu.VMEM((count, width), f32), pltpu.VMEM((count, width), f32)],
         grant=max(8, count // 6),
     )
     sums = call(

time: 59.1 us -> 58.9 us (level)
  starting transfers between devices: 20.1 us -> 19.4 us
    ppermute x13, starting transfers between devices: 8.76 us -> 7.9 us  [inward(): return lax.ppermute(x, 'ctx', pairs)]
    pallas_call x13 -> x14, Pallas kernels: 4.75 us -> 5.07 us  [call(): pl.pallas_call(body, out_shape=outs, in_specs=[VMEM] * len(operands), out...]
  transfers between devices with their start and end apart: 21 -> 21, of which waited for: 13 -> 14; matrix products, arithmetic and copies ran while one was open for 0% -> 0% of each run, Pallas kernels for 0% -> 1%
where the time goes in v1:
time: 58.9 us; the launch traced here: 58.7 us
  waiting for transfers between devices  22.2 us (38%)
  starting transfers between devices  19.4 us (33%)
  blocking collectives  11 us (19%)
  Pallas kernels  5.07 us (9%)
  between operations  0.94 us (2%)
    ppermute x13, waiting for transfers between devices, inward(): return lax.ppermute(x, 'ctx', pairs)  12.8 us
    ppermute x8, starting transfers between devices, outward(): return lax.ppermute(x, 'ctx', pairs)  11.5 us
    all_to_all x1, blocking collectives, local(): lax.all_to_all(sums, 'ctx', split_axis=0, concat_axis=0, tiled=True, axis...  11 us
    ppermute x8, waiting for transfers between devices, outward(): return lax.ppermute(x, 'ctx', pairs)  9.36 us
    ppermute x13, starting transfers between devices, inward(): return lax.ppermute(x, 'ctx', pairs)  7.9 us
    pallas_call x14, Pallas kernels, call(): pl.pallas_call(body, out_shape=outs, in_specs=[VMEM] * len(operands), out...  5.07 us
  transfers between devices with their start and end apart: 21, of which 14 were waited for; matrix products, arithmetic and copies ran while one was open for 0% of the time, Pallas kernels for 1%

profile of v1, /device:TPU:0, one launch (start us, length us, event | category | flops | bytes accessed | tf_op | source)
XLA Modules:
  0.0 58.7 jit_solution(10084896386418749812)
XLA Ops:
  1.1 3.1 %collective-permute-start = (bf16[40,128]{1,0:T(8,128)(2,1)S(1)}, bf16[40,128]{1,0:T(8,128)(2,1)S(1)}, u32[]{:S(2)}, u32[]{:S(2)}) collective-permute-start(bf16[40,128]{1,0:T(8,128)(2,1)S(1)} %get-tuple-element.37), channel_id=1, source_target_pairs={{0,4},{1,5},{2,6},{3,7},{4,0},{5,1},{6,2},{7,3},{8,12},{9,13},{10,... | collective-permute-start | bytes 30728 | tf_op jit(solution)/shard_map/ppermute | solution.py:386
  4.2 2.6 %collective-permute-start.1 = (bf16[40,128]{1,0:T(8,128)(2,1)S(1)}, bf16[40,128]{1,0:T(8,128)(2,1)S(1)}, u32[]{:S(2)}, u32[]{:S(2)}) collective-permute-start(bf16[40,128]{1,0:T(8,128)(2,1)S(1)} %get-tuple-element.38), channel_id=1, source_target_pairs={{0,8},{1,9},{2,10},{3,11},{4,12},{5,13},{6,14},{7,15},{8,0},{9,1},... | collective-permute-start | bytes 30728 | tf_op jit(solution)/shard_map/ppermute | solution.py:386
  6.8 0.9 %collective-permute-start.6 = (bf16[256,128]{1,0:T(8,128)(2,1)S(1)}, bf16[256,128]{1,0:T(8,128)(2,1)S(1)}, u32[]{:S(2)}, u32[]{:S(2)}) collective-permute-start(bf16[256,128]{1,0:T(8,128)(2,1)S(1)} %get-tuple-element.42), channel_id=1, source_target_pairs={{0,4},{1,5},{2,6},{3,7},{4,0},{5,1},{6,2},{7,3},{8,12},{9,13},{10,... | collective-permute-start | bytes 196616 | tf_op jit(solution)/shard_map/ppermute | solution.py:386
  7.8 3.5 %collective-permute-start.7 = (bf16[256,128]{1,0:T(8,128)(2,1)S(1)}, bf16[256,128]{1,0:T(8,128)(2,1)S(1)}, u32[]{:S(2)}, u32[]{:S(2)}) collective-permute-start(bf16[256,128]{1,0:T(8,128)(2,1)S(1)} %get-tuple-element.43), channel_id=1, source_target_pairs={{0,8},{1,9},{2,10},{3,11},{4,12},{5,13},{6,14},{7,15},{8,0},{9,1},... | collective-permute-start | bytes 196616 | tf_op jit(solution)/shard_map/ppermute | solution.py:386
  11.3 0.9 %collective-permute-done.2.refs_3_.refs_4_ = bf16[40,128]{1,0:T(8,128)(2,1)S(1)} collective-permute-done((bf16[40,128]{1,0:T(8,128)(2,1)S(1)}, bf16[40,128]{1,0:T(8,128)(2,1)S(1)}, u32[]{:S(2)}, u32[]{:S(2)}) %collective-permute-start.2) | collective-permute-done | bytes 10272 | tf_op jit(solution)/shard_map/ppermute | solution.py:386
  12.3 1.6 %collective-permute-start.4 = (bf16[112,128]{1,0:T(8,128)(2,1)S(1)}, bf16[112,128]{1,0:T(8,128)(2,1)S(1)}, u32[]{:S(2)}, u32[]{:S(2)}) collective-permute-start(bf16[112,128]{1,0:T(8,128)(2,1)S(1)} %shard_map.138.refs_0_.refs_9_), channel_id=1, source_target_pairs={{0,2},{1,3},{2,0},{3,1},{4,6},{5,7},{6,4},{7,5},{8,10},{9,11},{10,... | collective-permute-start | bytes 86024 | tf_op jit(solution)/shard_map/ppermute | solution.py:390
  13.9 1.9 %collective-permute-done.5.refs_3_.refs_12_ = bf16[112,128]{1,0:T(8,128)(2,1)S(1)} collective-permute-done((bf16[112,128]{1,0:T(8,128)(2,1)S(1)}, bf16[112,128]{1,0:T(8,128)(2,1)S(1)}, u32[]{:S(2)}, u32[]{:S(2)}) %collective-permute-start.5) | collective-permute-done | bytes 28704 | tf_op jit(solution)/shard_map/ppermute | solution.py:390
  16.0 0.3 collective-permute-done.4.refs_2_.refs_11_
  16.3 0.8 %collective-permute-done.3.refs_1_.refs_10_ = bf16[112,128]{1,0:T(8,128)(2,1)S(1)} collective-permute-done((bf16[112,128]{1,0:T(8,128)(2,1)S(1)}, bf16[112,128]{1,0:T(8,128)(2,1)S(1)}, u32[]{:S(2)}, u32[]{:S(2)}) %collective-permute-start.3) | collective-permute-done | bytes 28704 | tf_op jit(solution)/shard_map/ppermute | solution.py:390
  17.0 0.3 collective-permute-done.8.refs_8_
  17.3 1.1 %shard_map.141 = (bf16[112,128]{1,0:T(8,128)(2,1)S(1)}, bf16[112,128]{1,0:T(8,128)(2,1)S(1)}, bf16[112,128]{1,0:T(8,128)(2,1)S(1)}, bf16[112,128]{1,0:T(8,128)(2,1)S(1)}) custom-call(bf16[384,384]{1,0:T(8,128)(2,1)S(1)} %get-tuple-element.40.refs_0_, bf16[40,128]{1,0:T(8,128)(2,1)S(1)} %get-tuple-element.36.refs_0_.refs_1_, ...), custom_call_target="tpu_custom_call" | custom-call | flops 1000000000 | bytes 1000000 | tf_op jit(solution)/shard_map/pallas_call | solution.py:30
  18.5 1.6 %collective-permute-start.10 = (bf16[112,128]{1,0:T(8,128)(2,1)S(1)}, bf16[112,128]{1,0:T(8,128)(2,1)S(1)}, u32[]{:S(2)}, u32[]{:S(2)}) collective-permute-start(bf16[112,128]{1,0:T(8,128)(2,1)S(1)} %get-tuple-element.47), channel_id=1, source_target_pairs={{0,2},{1,3},{2,0},{3,1},{4,6},{5,7},{6,4},{7,5},{8,10},{9,11},{10,... | collective-permute-start | bytes 86024 | tf_op jit(solution)/shard_map/ppermute | solution.py:390
  20.1 0.3 collective-permute-start.11
  20.4 2.1 %collective-permute-done.10.refs_2_ = bf16[112,128]{1,0:T(8,128)(2,1)S(1)} collective-permute-done((bf16[112,128]{1,0:T(8,128)(2,1)S(1)}, bf16[112,128]{1,0:T(8,128)(2,1)S(1)}, u32[]{:S(2)}, u32[]{:S(2)}) %collective-permute-start.10) | collective-permute-done | bytes 28704 | tf_op jit(solution)/shard_map/ppermute | solution.py:390
  22.4 0.9 %collective-permute-done.11.refs_3_ = bf16[112,128]{1,0:T(8,128)(2,1)S(1)} collective-permute-done((bf16[112,128]{1,0:T(8,128)(2,1)S(1)}, bf16[112,128]{1,0:T(8,128)(2,1)S(1)}, u32[]{:S(2)}, u32[]{:S(2)}) %collective-permute-start.11) | collective-permute-done | bytes 28704 | tf_op jit(solution)/shard_map/ppermute | solution.py:390
  23.4 0.8 %shard_map.142 = (f32[48,512]{1,0:T(8,128)S(1)}, bf16[48,512]{1,0:T(8,128)(2,1)S(1)}, bf16[48,512]{1,0:T(8,128)(2,1)S(1)}, bf16[48,512]{1,0:T(8,128)(2,1)S(1)}) custom-call(bf16[112,128]{1,0:T(8,128)(2,1)S(1)} %get-tuple-element.45.refs_0_, bf16[112,128]{1,0:T(8,128)(2,1)S(1)} %collective-permute-done.9.refs_1_, ...), custom_call_target="tpu_custom_call" | custom-call | flops 1000000000 | bytes 1000000 | tf_op jit(solution)/shard_map/pallas_call | solution.py:30
  24.4 0.8 %collective-permute-start.13 = (bf16[48,512]{1,0:T(8,128)(2,1)S(1)}, bf16[48,512]{1,0:T(8,128)(2,1)S(1)}, u32[]{:S(2)}, u32[]{:S(2)}) collective-permute-start(bf16[48,512]{1,0:T(8,128)(2,1)S(1)} %get-tuple-element.51), channel_id=1, source_target_pairs={{0,2},{1,3},{2,0},{3,1},{4,6},{5,7},{6,4},{7,5},{8,10},{9,11},{10,... | collective-permute-start | bytes 147464 | tf_op jit(solution)/shard_map/ppermute | solution.py:390
  25.2 0.9 %collective-permute-start.14 = (bf16[48,512]{1,0:T(8,128)(2,1)S(1)}, bf16[48,512]{1,0:T(8,128)(2,1)S(1)}, u32[]{:S(2)}, u32[]{:S(2)}) collective-permute-start(bf16[48,512]{1,0:T(8,128)(2,1)S(1)} %get-tuple-element.52), channel_id=1, source_target_pairs={{0,3},{1,2},{2,1},{3,0},{4,7},{5,6},{6,5},{7,4},{8,11},{9,10},{10,... | collective-permute-start | bytes 147464 | tf_op jit(solution)/shard_map/ppermute | solution.py:390
  26.1 2.7 %collective-permute-done.13.refs_1_ = bf16[48,512]{1,0:T(8,128)(2,1)S(1)} collective-permute-done((bf16[48,512]{1,0:T(8,128)(2,1)S(1)}, bf16[48,512]{1,0:T(8,128)(2,1)S(1)}, u32[]{:S(2)}, u32[]{:S(2)}) %collective-permute-start.13) | collective-permute-done | bytes 49184 | tf_op jit(solution)/shard_map/ppermute | solution.py:390
  28.8 0.4 collective-permute-done.14.refs_2_
  29.3 4.1 %collective-permute-done.15.refs_0_ = bf16[48,512]{1,0:T(8,128)(2,1)S(1)} collective-permute-done((bf16[48,512]{1,0:T(8,128)(2,1)S(1)}, bf16[48,512]{1,0:T(8,128)(2,1)S(1)}, u32[]{:S(2)}, u32[]{:S(2)}) %collective-permute-start.15) | collective-permute-done | bytes 49184 | tf_op jit(solution)/shard_map/ppermute | solution.py:386
  33.4 1.3 %collective-permute-start.16 = (bf16[48,512]{1,0:T(8,128)(2,1)S(1)}, bf16[48,512]{1,0:T(8,128)(2,1)S(1)}, u32[]{:S(2)}, u32[]{:S(2)}) collective-permute-start(bf16[48,512]{1,0:T(8,128)(2,1)S(1)} %get-tuple-element.56), channel_id=1, source_target_pairs={{0,8},{1,9},{2,10},{3,11},{4,12},{5,13},{6,14},{7,15},{8,0},{9,1},... | collective-permute-start | bytes 147464 | tf_op jit(solution)/shard_map/ppermute | solution.py:386
  34.7 4.1 %collective-permute-done.16.refs_0_ = bf16[48,512]{1,0:T(8,128)(2,1)S(1)} collective-permute-done((bf16[48,512]{1,0:T(8,128)(2,1)S(1)}, bf16[48,512]{1,0:T(8,128)(2,1)S(1)}, u32[]{:S(2)}, u32[]{:S(2)}) %collective-permute-start.16) | collective-permute-done | bytes 49184 | tf_op jit(solution)/shard_map/ppermute | solution.py:386
  39.0 1.1 %collective-permute-start.19 = (bf16[48,512]{1,0:T(8,128)(2,1)S(1)}, bf16[48,512]{1,0:T(8,128)(2,1)S(1)}, u32[]{:S(2)}, u32[]{:S(2)}) collective-permute-start(bf16[48,512]{1,0:T(8,128)(2,1)S(1)} %get-tuple-element.58), channel_id=1, source_target_pairs={{0,3},{1,2},{2,1},{3,0},{4,7},{5,6},{6,5},{7,4},{8,11},{9,10},{10,... | collective-permute-start | bytes 147464 | tf_op jit(solution)/shard_map/ppermute | solution.py:390
  40.1 1.1 %collective-permute-start.18 = (bf16[48,512]{1,0:T(8,128)(2,1)S(1)}, bf16[48,512]{1,0:T(8,128)(2,1)S(1)}, u32[]{:S(2)}, u32[]{:S(2)}) collective-permute-start(bf16[48,512]{1,0:T(8,128)(2,1)S(1)} %get-tuple-element.58), channel_id=1, source_target_pairs={{0,2},{1,3},{2,0},{3,1},{4,6},{5,7},{6,4},{7,5},{8,10},{9,11},{10,... | collective-permute-start | bytes 147464 | tf_op jit(solution)/shard_map/ppermute | solution.py:390
  41.2 0.7 %shard_map.146 = (f32[48,768]{1,0:T(8,128)S(1)}, f32[48,768]{1,0:T(8,128)S(1)}, f32[48,128]{1,0:T(8,128)S(1)}) custom-call(bf16[1,2048,768]{2,1,0:T(8,128)(2,1)S(1)} %copy-done, bf16[1,2048,768]{2,1,0:T(8,128)(2,1)S(1)} %copy-done.1, bf16[1,2048]{1,0:T(2,128)(2,1)S(1)} %reshape.3.gain, f32[48,512]{1,0:T(8,128)S(1)} %get-tuple-element.57.refs_0_, ...), custom_call_target="tpu_custom_call" | custom-call | flops 1000000000 | bytes 1000000 | tf_op jit(solution)/shard_map/pallas_call | solution.py:30
  41.9 0.7 %collective-permute-done.19.refs_3_ = bf16[48,512]{1,0:T(8,128)(2,1)S(1)} collective-permute-done((bf16[48,512]{1,0:T(8,128)(2,1)S(1)}, bf16[48,512]{1,0:T(8,128)(2,1)S(1)}, u32[]{:S(2)}, u32[]{:S(2)}) %collective-permute-start.19) | collective-permute-done | bytes 49184 | tf_op jit(solution)/shard_map/ppermute | solution.py:390
  42.6 1.7 %collective-permute-done.18.refs_2_ = bf16[48,512]{1,0:T(8,128)(2,1)S(1)} collective-permute-done((bf16[48,512]{1,0:T(8,128)(2,1)S(1)}, bf16[48,512]{1,0:T(8,128)(2,1)S(1)}, u32[]{:S(2)}, u32[]{:S(2)}) %collective-permute-start.18) | collective-permute-done | bytes 49184 | tf_op jit(solution)/shard_map/ppermute | solution.py:390
  44.3 1.3 %shard_map.147 = (f32[24,2048]{1,0:T(8,128)S(1)}, bf16[24,2048]{1,0:T(8,128)(2,1)S(1)}, f32[3,2048]{1,0:T(4,128)S(1)}) custom-call(bf16[1,2048,768]{2,1,0:T(8,128)(2,1)S(1)} %copy-done, bf16[1,2048,768]{2,1,0:T(8,128)(2,1)S(1)} %copy-done.1, bf16[1,768,2048]{2,1,0:T(8,128)(2,1)S(1)} %copy-done.2, bf16[1,2048]{1,0:T(2,128)(2,1)S(1)} %reshape.3.gain, ...), custom_call_target="tpu_custom_call" | custom-call | flops 1000000000 | bytes 1000000 | tf_op jit(solution)/shard_map/pallas_call | solution.py:30
  45.6 1.3 %collective-permute-done.20.other = bf16[24,2048]{1,0:T(8,128)(2,1)S(1)} collective-permute-done((bf16[24,2048]{1,0:T(8,128)(2,1)S(1)}, bf16[24,2048]{1,0:T(8,128)(2,1)S(1)}, u32[]{:S(2)}, u32[]{:S(2)}) %collective-permute-start.20) | collective-permute-done | bytes 98336 | tf_op jit(solution)/shard_map/ppermute | solution.py:390
  47.0 11.0 %all_to_all.5.back = bf16[8,48,128]{2,1,0:T(8,128)(2,1)S(1)} all-to-all(bf16[8,48,128]{2,1,0:T(8,128)(2,1)S(1)} %shard_map.148), channel_id=1, replica_groups={{0,2,4,6,8,10,12,14},{1,3,5,7,9,11,13,15},{16,18,20,22,24,26,28,30},{17..., dimensions={0} | all-to-all | bytes 196608 | tf_op jit(solution)/shard_map/all_to_all | solution.py:490
  58.0 0.6 %shard_map.149 = bf16[3,2048]{1,0:T(4,128)(2,1)} custom-call(f32[3,2048]{1,0:T(4,128)S(1)} %get-tuple-element.62.state, bf16[8,48,128]{2,1,0:T(8,128)(2,1)S(1)} %all_to_all.5.back), custom_call_target="tpu_custom_call" | custom-call | flops 1000000000 | bytes 1000000 | tf_op jit(solution)/shard_map/pallas_call | solution.py:30
  (52 shorter events, 1.3 us)
Async XLA Ops:
  0.0 0.9 %copy-start.9 = (bf16[3,512]{1,0:T(4,128)(2,1)S(1)}, bf16[3,512]{1,0:T(4,128)(2,1)}, u32[]{:S(2)}) copy-start(bf16[3,512]{1,0:T(4,128)(2,1)} %new_values.1) | copy-start | bytes 9220
  0.0 0.9 %copy-start.8 = (bf16[3,512]{1,0:T(4,128)(2,1)S(1)}, bf16[3,512]{1,0:T(4,128)(2,1)}, u32[]{:S(2)}) copy-start(bf16[3,512]{1,0:T(4,128)(2,1)} %new_keys.1) | copy-start | bytes 9220
  0.0 0.9 %copy-start.6 = (bf16[3,4096]{1,0:T(4,128)(2,1)S(1)}, bf16[3,4096]{1,0:T(4,128)(2,1)}, u32[]{:S(2)}) copy-start(bf16[3,4096]{1,0:T(4,128)(2,1)} %queries.1) | copy-start | bytes 73732
  0.0 6.7 %copy-start.5 = (bf16[128,512]{1,0:T(8,128)(2,1)S(1)}, bf16[128,512]{1,0:T(8,128)(2,1)}, u32[]{:S(2)}) copy-start(bf16[128,512]{1,0:T(8,128)(2,1)} %values.1) | copy-start | bytes 393220
  0.0 6.7 %copy-start.4 = (bf16[128,512]{1,0:T(8,128)(2,1)S(1)}, bf16[128,512]{1,0:T(8,128)(2,1)}, u32[]{:S(2)}) copy-start(bf16[128,512]{1,0:T(8,128)(2,1)} %keys.1) | copy-start | bytes 393220
  1.1 10.2 %collective-permute-start = (bf16[40,128]{1,0:T(8,128)(2,1)S(1)}, bf16[40,128]{1,0:T(8,128)(2,1)S(1)}, u32[]{:S(2)}, u32[]{:S(2)}) collective-permute-start(bf16[40,128]{1,0:T(8,128)(2,1)S(1)} %get-tuple-element.37), channel_id=1, source_target_pairs={{0,4},{1,5},{2,6},{3,7},{4,0},{5,1},{6,2},{7,3},{8,12},{9,13},{10,... | collective-permute-start | bytes 30728 | tf_op jit(solution)/shard_map/ppermute | solution.py:386
  4.2 7.1 %collective-permute-start.1 = (bf16[40,128]{1,0:T(8,128)(2,1)S(1)}, bf16[40,128]{1,0:T(8,128)(2,1)S(1)}, u32[]{:S(2)}, u32[]{:S(2)}) collective-permute-start(bf16[40,128]{1,0:T(8,128)(2,1)S(1)} %get-tuple-element.38), channel_id=1, source_target_pairs={{0,8},{1,9},{2,10},{3,11},{4,12},{5,13},{6,14},{7,15},{8,0},{9,1},... | collective-permute-start | bytes 30728 | tf_op jit(solution)/shard_map/ppermute | solution.py:386
  6.8 5.5 %collective-permute-start.2 = (bf16[40,128]{1,0:T(8,128)(2,1)S(1)}, bf16[40,128]{1,0:T(8,128)(2,1)S(1)}, u32[]{:S(2)}, u32[]{:S(2)}) collective-permute-start(bf16[40,128]{1,0:T(8,128)(2,1)S(1)} %get-tuple-element.39), channel_id=1, source_target_pairs={{0,12},{1,13},{2,14},{3,15},{4,8},{5,9},{6,10},{7,11},{8,4},{9,5},... | collective-permute-start | bytes 30728 | tf_op jit(solution)/shard_map/ppermute | solution.py:386
  6.8 10.2 %collective-permute-start.6 = (bf16[256,128]{1,0:T(8,128)(2,1)S(1)}, bf16[256,128]{1,0:T(8,128)(2,1)S(1)}, u32[]{:S(2)}, u32[]{:S(2)}) collective-permute-start(bf16[256,128]{1,0:T(8,128)(2,1)S(1)} %get-tuple-element.42), channel_id=1, source_target_pairs={{0,4},{1,5},{2,6},{3,7},{4,0},{5,1},{6,2},{7,3},{8,12},{9,13},{10,... | collective-permute-start | bytes 196616 | tf_op jit(solution)/shard_map/ppermute | solution.py:386
  7.8 9.3 %collective-permute-start.7 = (bf16[256,128]{1,0:T(8,128)(2,1)S(1)}, bf16[256,128]{1,0:T(8,128)(2,1)S(1)}, u32[]{:S(2)}, u32[]{:S(2)}) collective-permute-start(bf16[256,128]{1,0:T(8,128)(2,1)S(1)} %get-tuple-element.43), channel_id=1, source_target_pairs={{0,8},{1,9},{2,10},{3,11},{4,12},{5,13},{6,14},{7,15},{8,0},{9,1},... | collective-permute-start | bytes 196616 | tf_op jit(solution)/shard_map/ppermute | solution.py:386
  11.3 6.1 %collective-permute-start.8 = (bf16[256,128]{1,0:T(8,128)(2,1)S(1)}, bf16[256,128]{1,0:T(8,128)(2,1)S(1)}, u32[]{:S(2)}, u32[]{:S(2)}) collective-permute-start(bf16[256,128]{1,0:T(8,128)(2,1)S(1)} %get-tuple-element.44), channel_id=1, source_target_pairs={{0,12},{1,13},{2,14},{3,15},{4,8},{5,9},{6,10},{7,11},{8,4},{9,5},... | collective-permute-start | bytes 196616 | tf_op jit(solution)/shard_map/ppermute | solution.py:386
  12.2 11.2 %copy-start.3 = (bf16[256,2048]{1,0:T(8,128)(2,1)S(1)}, bf16[256,2048]{1,0:T(8,128)(2,1)}, u32[]{:S(2)}) copy-start(bf16[256,2048]{1,0:T(8,128)(2,1)} %refs_4_.1) | copy-start | bytes 3145732
  12.2 11.2 %copy-start.7 = (bf16[3,2048]{1,0:T(4,128)(2,1)S(1)}, bf16[3,2048]{1,0:T(4,128)(2,1)}, u32[]{:S(2)}) copy-start(bf16[3,2048]{1,0:T(4,128)(2,1)} %refs_5_.1) | copy-start | bytes 36868
  12.2 3.6 %collective-permute-start.5 = (bf16[112,128]{1,0:T(8,128)(2,1)S(1)}, bf16[112,128]{1,0:T(8,128)(2,1)S(1)}, u32[]{:S(2)}, u32[]{:S(2)}) collective-permute-start(bf16[112,128]{1,0:T(8,128)(2,1)S(1)} %shard_map.138.refs_0_.refs_9_), channel_id=1, source_target_pairs={{0,3},{1,2},{2,1},{3,0},{4,7},{5,6},{6,5},{7,4},{8,11},{9,10},{10,... | collective-permute-start | bytes 86024 | tf_op jit(solution)/shard_map/ppermute | solution.py:390
  12.3 3.9 %collective-permute-start.4 = (bf16[112,128]{1,0:T(8,128)(2,1)S(1)}, bf16[112,128]{1,0:T(8,128)(2,1)S(1)}, u32[]{:S(2)}, u32[]{:S(2)}) collective-permute-start(bf16[112,128]{1,0:T(8,128)(2,1)S(1)} %shard_map.138.refs_0_.refs_9_), channel_id=1, source_target_pairs={{0,2},{1,3},{2,0},{3,1},{4,6},{5,7},{6,4},{7,5},{8,10},{9,11},{10,... | collective-permute-start | bytes 86024 | tf_op jit(solution)/shard_map/ppermute | solution.py:390
  15.8 1.2 %collective-permute-start.3 = (bf16[112,128]{1,0:T(8,128)(2,1)S(1)}, bf16[112,128]{1,0:T(8,128)(2,1)S(1)}, u32[]{:S(2)}, u32[]{:S(2)}) collective-permute-start(bf16[112,128]{1,0:T(8,128)(2,1)S(1)} %shard_map.138.refs_0_.refs_9_), channel_id=1, source_target_pairs={{0,1},{1,0},{2,3},{3,2},{4,5},{5,4},{6,7},{7,6},{8,9},{9,8},{10,11... | collective-permute-start | bytes 86024 | tf_op jit(solution)/shard_map/ppermute | solution.py:390
  18.5 1.9 %collective-permute-start.9 = (bf16[112,128]{1,0:T(8,128)(2,1)S(1)}, bf16[112,128]{1,0:T(8,128)(2,1)S(1)}, u32[]{:S(2)}, u32[]{:S(2)}) collective-permute-start(bf16[112,128]{1,0:T(8,128)(2,1)S(1)} %get-tuple-element.46), channel_id=1, source_target_pairs={{0,1},{1,0},{2,3},{3,2},{4,5},{5,4},{6,7},{7,6},{8,9},{9,8},{10,11... | collective-permute-start | bytes 86024 | tf_op jit(solution)/shard_map/ppermute | solution.py:390
  18.5 3.9 %collective-permute-start.10 = (bf16[112,128]{1,0:T(8,128)(2,1)S(1)}, bf16[112,128]{1,0:T(8,128)(2,1)S(1)}, u32[]{:S(2)}, u32[]{:S(2)}) collective-permute-start(bf16[112,128]{1,0:T(8,128)(2,1)S(1)} %get-tuple-element.47), channel_id=1, source_target_pairs={{0,2},{1,3},{2,0},{3,1},{4,6},{5,7},{6,4},{7,5},{8,10},{9,11},{10,... | collective-permute-start | bytes 86024 | tf_op jit(solution)/shard_map/ppermute | solution.py:390
  20.1 3.3 %collective-permute-start.11 = (bf16[112,128]{1,0:T(8,128)(2,1)S(1)}, bf16[112,128]{1,0:T(8,128)(2,1)S(1)}, u32[]{:S(2)}, u32[]{:S(2)}) collective-permute-start(bf16[112,128]{1,0:T(8,128)(2,1)S(1)} %get-tuple-element.48), channel_id=1, source_target_pairs={{0,3},{1,2},{2,1},{3,0},{4,7},{5,6},{6,5},{7,4},{8,11},{9,10},{10,... | collective-permute-start | bytes 86024 | tf_op jit(solution)/shard_map/ppermute | solution.py:390
  24.2 1.9 %collective-permute-start.12 = (bf16[48,512]{1,0:T(8,128)(2,1)S(1)}, bf16[48,512]{1,0:T(8,128)(2,1)S(1)}, u32[]{:S(2)}, u32[]{:S(2)}) collective-permute-start(bf16[48,512]{1,0:T(8,128)(2,1)S(1)} %get-tuple-element.50), channel_id=1, source_target_pairs={{0,1},{1,0},{2,3},{3,2},{4,5},{5,4},{6,7},{7,6},{8,9},{9,8},{10,11... | collective-permute-start | bytes 147464 | tf_op jit(solution)/shard_map/ppermute | solution.py:390
  24.4 4.4 %collective-permute-start.13 = (bf16[48,512]{1,0:T(8,128)(2,1)S(1)}, bf16[48,512]{1,0:T(8,128)(2,1)S(1)}, u32[]{:S(2)}, u32[]{:S(2)}) collective-permute-start(bf16[48,512]{1,0:T(8,128)(2,1)S(1)} %get-tuple-element.51), channel_id=1, source_target_pairs={{0,2},{1,3},{2,0},{3,1},{4,6},{5,7},{6,4},{7,5},{8,10},{9,11},{10,... | collective-permute-start | bytes 147464 | tf_op jit(solution)/shard_map/ppermute | solution.py:390
  25.2 4.0 %collective-permute-start.14 = (bf16[48,512]{1,0:T(8,128)(2,1)S(1)}, bf16[48,512]{1,0:T(8,128)(2,1)S(1)}, u32[]{:S(2)}, u32[]{:S(2)}) collective-permute-start(bf16[48,512]{1,0:T(8,128)(2,1)S(1)} %get-tuple-element.52), channel_id=1, source_target_pairs={{0,3},{1,2},{2,1},{3,0},{4,7},{5,6},{6,5},{7,4},{8,11},{9,10},{10,... | collective-permute-start | bytes 147464 | tf_op jit(solution)/shard_map/ppermute | solution.py:390
  29.3 4.2 %collective-permute-start.15 = (bf16[48,512]{1,0:T(8,128)(2,1)S(1)}, bf16[48,512]{1,0:T(8,128)(2,1)S(1)}, u32[]{:S(2)}, u32[]{:S(2)}) collective-permute-start(bf16[48,512]{1,0:T(8,128)(2,1)S(1)} %get-tuple-element.54), channel_id=1, source_target_pairs={{0,4},{1,5},{2,6},{3,7},{4,0},{5,1},{6,2},{7,3},{8,12},{9,13},{10,... | collective-permute-start | bytes 147464 | tf_op jit(solution)/shard_map/ppermute | solution.py:386
  33.4 5.4 %copy-start.12 = (bf16[2048]{0:T(1024)(128)(2,1)S(1)}, bf16[2048]{0:T(1024)(128)(2,1)}, u32[]{:S(2)}) copy-start(bf16[2048]{0:T(1024)(128)(2,1)} %param.22) | copy-start | bytes 12292
  33.4 7.8 %copy-start = (bf16[1,2048,768]{2,1,0:T(8,128)(2,1)S(1)}, bf16[1,2048,768]{2,1,0:T(8,128)(2,1)}, u32[]{:S(2)}) copy-start(bf16[1,2048,768]{2,1,0:T(8,128)(2,1)} %gate.3) | copy-start | bytes 9437188
  33.4 7.8 %copy-start.1 = (bf16[1,2048,768]{2,1,0:T(8,128)(2,1)S(1)}, bf16[1,2048,768]{2,1,0:T(8,128)(2,1)}, u32[]{:S(2)}) copy-start(bf16[1,2048,768]{2,1,0:T(8,128)(2,1)} %up.3) | copy-start | bytes 9437188
  33.4 5.3 %collective-permute-start.16 = (bf16[48,512]{1,0:T(8,128)(2,1)S(1)}, bf16[48,512]{1,0:T(8,128)(2,1)S(1)}, u32[]{:S(2)}, u32[]{:S(2)}) collective-permute-start(bf16[48,512]{1,0:T(8,128)(2,1)S(1)} %get-tuple-element.56), channel_id=1, source_target_pairs={{0,8},{1,9},{2,10},{3,11},{4,12},{5,13},{6,14},{7,15},{8,0},{9,1},... | collective-permute-start | bytes 147464 | tf_op jit(solution)/shard_map/ppermute | solution.py:386
  38.8 2.4 %collective-permute-start.17 = (bf16[48,512]{1,0:T(8,128)(2,1)S(1)}, bf16[48,512]{1,0:T(8,128)(2,1)S(1)}, u32[]{:S(2)}, u32[]{:S(2)}) collective-permute-start(bf16[48,512]{1,0:T(8,128)(2,1)S(1)} %get-tuple-element.58), channel_id=1, source_target_pairs={{0,1},{1,0},{2,3},{3,2},{4,5},{5,4},{6,7},{7,6},{8,9},{9,8},{10,11... | collective-permute-start | bytes 147464 | tf_op jit(solution)/shard_map/ppermute | solution.py:390
  39.0 3.6 %collective-permute-start.19 = (bf16[48,512]{1,0:T(8,128)(2,1)S(1)}, bf16[48,512]{1,0:T(8,128)(2,1)S(1)}, u32[]{:S(2)}, u32[]{:S(2)}) collective-permute-start(bf16[48,512]{1,0:T(8,128)(2,1)S(1)} %get-tuple-element.58), channel_id=1, source_target_pairs={{0,3},{1,2},{2,1},{3,0},{4,7},{5,6},{6,5},{7,4},{8,11},{9,10},{10,... | collective-permute-start | bytes 147464 | tf_op jit(solution)/shard_map/ppermute | solution.py:390
  40.1 4.2 %collective-permute-start.18 = (bf16[48,512]{1,0:T(8,128)(2,1)S(1)}, bf16[48,512]{1,0:T(8,128)(2,1)S(1)}, u32[]{:S(2)}, u32[]{:S(2)}) collective-permute-start(bf16[48,512]{1,0:T(8,128)(2,1)S(1)} %get-tuple-element.58), channel_id=1, source_target_pairs={{0,2},{1,3},{2,0},{3,1},{4,6},{5,7},{6,4},{7,5},{8,10},{9,11},{10,... | collective-permute-start | bytes 147464 | tf_op jit(solution)/shard_map/ppermute | solution.py:390
  41.2 3.1 %copy-start.2 = (bf16[1,768,2048]{2,1,0:T(8,128)(2,1)S(1)}, bf16[1,768,2048]{2,1,0:T(8,128)(2,1)}, u32[]{:S(2)}) copy-start(bf16[1,768,2048]{2,1,0:T(8,128)(2,1)} %down.1) | copy-start | bytes 9437188
  45.6 1.4 %collective-permute-start.20 = (bf16[24,2048]{1,0:T(8,128)(2,1)S(1)}, bf16[24,2048]{1,0:T(8,128)(2,1)S(1)}, u32[]{:S(2)}, u32[]{:S(2)}) collective-permute-start(bf16[24,2048]{1,0:T(8,128)(2,1)S(1)} %get-tuple-element.64), channel_id=1, source_target_pairs={{0,1},{1,0},{2,3},{3,2},{4,5},{5,4},{6,7},{7,6},{8,9},{9,8},{10,11... | collective-permute-start | bytes 294920 | tf_op jit(solution)/shard_map/ppermute | solution.py:390
  (2 other events, 1.7 us)

commit v2 on v1

--- a/solution.py
+++ b/solution.py
@@ -42,15 +42,15 @@
     return jnp.right_shift(x * (-(-65536 // rows)), 16)
 
 
-def owners(position, half, rows):
-    odd = (position >= half).astype(jnp.int32)
-    rest = position - odd * half
-    pair = third(rest, rows)
-    return 2 * pair + odd, rest - pair * rows
-
-
-def place(shard, half, rows):
-    return jnp.bitwise_and(shard, 1) * half + jnp.right_shift(shard, 1) * rows
+def owners(position, outer, inner, rows):
+    b = third(position, outer * rows)
+    rest = position - b * (outer * rows)
+    a = third(rest, rows)
+    return a * inner + b, rest - a * rows
+
+
+def place(shard, outer, inner, rows):
+    return (lax.rem(shard, inner) * outer + shard // inner) * rows
 
 
 def stat_lines(lines):
@@ -116,7 +116,7 @@
     a, b = coordinates(inner)
     per_row = rows * GROUP
     position = lax.broadcasted_iota(jnp.int32, (count, 1), 0)
-    owner, row = owners(position, count // 2, rows)
+    owner, row = owners(position, outer, inner, rows)
     at_a = jnp.bitwise_xor(jnp.right_shift(owner, inner.bit_length() - 1), a)
     at_b = jnp.bitwise_xor(jnp.bitwise_and(owner, inner - 1), b)
     source = (at_b * outer + at_a) * per_row + row
@@ -158,7 +158,9 @@
         return jnp.where(usable, s.reshape((GROUP, count, keys.shape[0])), MASKED)
 
     fresh[...] = jnp.zeros_like(fresh)
-    owner, row = owners(lax.broadcasted_iota(jnp.int32, (count, 1), 0), count // 2, rows)
+    owner, row = owners(
+        lax.broadcasted_iota(jnp.int32, (count, 1), 0), outer, inner, rows
+    )
     position = owner * rows + row
     slot = lax.broadcasted_iota(jnp.int32, (count, outer * lines), 1)
     reach = jnp.full((count, outer * lines), -1, jnp.int32)
@@ -216,7 +218,7 @@
             ).astype(bf16)
 
 
-def project(inner, rows, count, heads, *refs):
+def project(outer, inner, rows, count, heads, *refs):
     chunks, (weight, residual), refs = refs[:inner], refs[inner : inner + 2], refs[inner + 2 :]
     own, outs, total = refs[0], refs[1:inner], refs[inner]
     _, b = coordinates(inner)
@@ -251,7 +253,7 @@
         )
         for h in range(heads)
     )
-    start = place(lax.axis_index("ctx"), count // 2, rows)
+    start = place(lax.axis_index("ctx"), outer, inner, rows)
     added = residual[...].astype(f32)
     for r in range(rows):
         row = pl.ds(start + r, 1)
@@ -271,9 +273,10 @@
     sent[...] = partial.astype(bf16)
 
 
-def route(outer, inner, rows, count, top, *refs):
+def route(outer, inner, rows, top, *refs):
     blocks, out = refs[:-1], refs[-1]
     a, b = coordinates(inner)
+    out[...] = jnp.zeros_like(out)
     expert = lax.axis_index("ctx").astype(f32)
     lane = lax.broadcasted_iota(jnp.int32, (outer, HEAD_DIM), 1)
     for m in range(inner):
@@ -286,7 +289,7 @@
             share = jnp.broadcast_to(share, (outer, LANES))
             for k in range(outer):
                 shard = jnp.bitwise_xor(a, k) * inner + jnp.bitwise_xor(b, m)
-                out[pl.ds(place(shard, count // 2, rows) + r, 1)] = share[k : k + 1]
+                out[pl.ds(place(shard, outer, inner, rows) + r, 1)] = share[k : k + 1]
 
 
 def begin(inner, gate, up, gain, *refs):
@@ -305,11 +308,13 @@
     squares[...] = total
 
 
-def expert(inner, early, rows, gate, up, down, gain, weights, begun_gate, begun_up, begun, *refs):
-    pieces, (kept, sent, mine, state, held) = refs[:inner], refs[inner:]
+def expert(
+    outer, inner, early, rows, gate, up, down, gain, weights, begun_gate, begun_up, begun, *refs
+):
+    pieces, refs = refs[:inner], refs[inner:]
+    kept, outs, (mine, state, held, dense) = refs[0], refs[1:inner], refs[inner:]
     _, b = coordinates(inner)
     columns = pieces[0].shape[1]
-    half = kept.shape[0]
     squares, gated, lifted = begun[:, 0:1], begun_gate[...], begun_up[...]
     for k, piece in enumerate(pieces):
         lanes = aligned(jnp.bitwise_xor(b, k), columns)
@@ -322,28 +327,40 @@
             lifted = lifted + jnp.dot(x, up[0, lanes], preferred_element_type=f32)
     scale = lax.rsqrt(squares * (1.0 / (inner * columns)) + epsilon)
     gated, lifted = gated * scale, lifted * scale
-    start = place(lax.axis_index("ctx"), half, rows)
+    start = place(lax.axis_index("ctx"), outer, inner, rows)
     for r in range(rows):
         mine[r : r + 1] = state[pl.ds(start + r, 1)]
     active = (gated / (1.0 + jnp.exp(-gated)) * lifted).astype(bf16)
     held[...] = jnp.dot(active, down[0], preferred_element_type=f32) * weights[:, 0:1]
-    odd = jnp.bitwise_and(b, 1)
-    kept[...] = held[aligned(odd, half)]
-    sent[...] = held[aligned(1 - odd, half)].astype(bf16)
-
-
-def join(rows, kept, other, out, total, dense):
-    total[...] = kept[...] + other[...].astype(f32)
-    for t in range(out.shape[0]):
-        for j in range(total.shape[1] // LANES):
-            dense[t, j * rows : (j + 1) * rows] = total[
-                t * rows : (t + 1) * rows, j * LANES : (j + 1) * LANES
+    block = outer * rows
+    for m in range(inner):
+        for j in range(held.shape[1] // LANES):
+            dense[m, j * block : (j + 1) * block] = held[
+                m * block : (m + 1) * block, j * LANES : (j + 1) * LANES
             ]
-    out[...] = dense[...].astype(bf16)
-
-
-def combine(rows, state, back, out, total):
-    total[...] = sum(back[t].astype(f32) for t in range(back.shape[0]))
+    kept[...] = dense[b]
+    for k in range(1, inner):
+        outs[k - 1][...] = dense[jnp.bitwise_xor(b, k)].astype(bf16)
+
+
+def join(outer, inner, rows, *refs):
+    kept, others, refs = refs[0], refs[1:inner], refs[inner:]
+    own, outs, (total, dense) = refs[0], refs[1:outer], refs[outer:]
+    a, _ = coordinates(inner)
+    total[...] = functools.reduce(lambda x, y: x + y[...].astype(f32), others, kept[...])
+    block = outer * rows
+    for t in range(outer):
+        for j in range(total.shape[0] // block):
+            at = j * block + t * rows
+            dense[t, j * rows : (j + 1) * rows] = total[at : at + rows]
+    own[...] = dense[a]
+    for k in range(1, outer):
+        outs[k - 1][...] = dense[jnp.bitwise_xor(a, k)].astype(bf16)
+
+
+def combine(rows, state, own, *refs):
+    others, (out, total) = refs[:-2], refs[-2:]
+    total[...] = functools.reduce(lambda x, y: x + y[...].astype(f32), others, own[...])
     for j in range(state.shape[1] // LANES):
         lanes = slice(j * LANES, (j + 1) * LANES)
         out[:, lanes] = (state[:, lanes] + total[j * rows : (j + 1) * rows]).astype(bf16)
@@ -370,8 +387,7 @@
     inner = shards // outer
     rows, width = residual_in.shape
     cache = cache_keys.shape[0]
-    half = -(-shards // 2 * rows // 8) * 8
-    count = 2 * half
+    count = -(-shards * rows // 16) * 16
     top = expert_ids.shape[1]
     step = out_weight.shape[0]
     heads = max(1, step // HEAD_DIM)
@@ -443,7 +459,7 @@
             jnp.zeros((HEAD_DIM, width), out_weight.dtype), out_weight, (at, 0)
         )
     kept, *parts = call(
-        functools.partial(project, inner, rows, count, heads),
+        functools.partial(project, outer, inner, rows, count, heads),
         [shape((count, columns), f32)] + [shape((count, columns))] * (inner - 1),
         (*chunks, out_weight, residual_in),
         [pltpu.VMEM((count, width), f32)],
@@ -459,7 +475,7 @@
     pieces = [kept] + exchange(inward, [sent] * inner)[1:]
 
     weights = call(
-        functools.partial(route, outer, inner, rows, count, top),
+        functools.partial(route, outer, inner, rows, top),
         shape((count, LANES), f32),
         wanted,
         flops=10**7,
@@ -472,28 +488,33 @@
         [hidden, hidden, shape((count, LANES), f32)],
         (expert_gate, expert_up, gain, *pieces[:early]),
     )
-    kept, sent, state = call(
-        functools.partial(expert, inner, early, rows),
-        [shape((half, width), f32), shape((half, width)), shape((rows, width), f32)],
+    gathered = (outer * lines, LANES)
+    kept, *rest = call(
+        functools.partial(expert, outer, inner, early, rows),
+        [shape(gathered, f32)]
+        + [shape(gathered)] * (inner - 1)
+        + [shape((rows, width), f32)],
         (expert_gate, expert_up, expert_down, gain, weights, *begun, *pieces),
-        [pltpu.VMEM((count, width), f32), pltpu.VMEM((count, width), f32)],
+        [
+            pltpu.VMEM((count, width), f32),
+            pltpu.VMEM((count, width), f32),
+            pltpu.VMEM((inner,) + gathered, f32),
+        ],
         grant=max(8, count // 6),
     )
-    sums = call(
-        functools.partial(join, rows),
-        shape((shards // 2, lines, LANES)),
-        (kept, inward(sent, 1)),
-        [pltpu.VMEM((half, width), f32), pltpu.VMEM((shards // 2, lines, LANES), f32)],
-        grant=max(4, count // 12),
-    )
-    parity = [[2 * t + odd for t in range(shards // 2)] for odd in range(2)]
-    back = lax.all_to_all(
-        sums, "ctx", split_axis=0, concat_axis=0, tiled=True, axis_index_groups=parity
-    )
+    state = rest.pop()
+    others = exchange(inward, [None] + rest)[1:]
+    own, *rest = call(
+        functools.partial(join, outer, inner, rows),
+        [shape((lines, LANES), f32)] + [shape((lines, LANES))] * (outer - 1),
+        (kept, *others),
+        [pltpu.VMEM(gathered, f32), pltpu.VMEM((outer, lines, LANES), f32)],
+    )
+    others = exchange(outward, [None] + rest)[1:]
     return call(
         functools.partial(combine, rows),
         shape((rows, width)),
-        (state, back),
+        (state, own, *others),
         [pltpu.VMEM((lines, LANES), f32)],
     )
 

time: 58.9 us -> 60 us (1.019)
  blocking collectives: 11 us -> 0 us
  starting transfers between devices: 19.4 us -> 25.7 us
  waiting for transfers between devices: 22.2 us -> 28.1 us
    all_to_all x1 -> x0, blocking collectives: 11 us -> none  [local(): lax.all_to_all(sums, 'ctx', split_axis=0, concat_axis=0, tiled=True, axis...]
    ppermute x8 -> x11, starting transfers between devices: 11.5 us -> 15.9 us  [outward(): return lax.ppermute(x, 'ctx', pairs)]
    ppermute x8 -> x11, waiting for transfers between devices: 9.36 us -> 13.4 us  [outward(): return lax.ppermute(x, 'ctx', pairs)]
    ppermute x13 -> x15, starting transfers between devices: 7.9 us -> 9.75 us  [inward(): return lax.ppermute(x, 'ctx', pairs)]
    ppermute x13 -> x15, waiting for transfers between devices: 12.8 us -> 14.7 us  [inward(): return lax.ppermute(x, 'ctx', pairs)]
  transfers between devices with their start and end apart: 21 -> 26, of which waited for: 14 -> 17; matrix products, arithmetic and copies ran while one was open for 0% -> 0% of each run, Pallas kernels for 1% -> 1%
where the time goes in v2:
time: 60 us; the launch traced here: 59.8 us
  waiting for transfers between devices  28.1 us (47%)
  starting transfers between devices  25.7 us (43%)
  Pallas kernels  5.05 us (8%)
  between operations  0.95 us (2%)
    ppermute x11, starting transfers between devices, outward(): return lax.ppermute(x, 'ctx', pairs)  15.9 us
    ppermute x15, waiting for transfers between devices, inward(): return lax.ppermute(x, 'ctx', pairs)  14.7 us
    ppermute x11, waiting for transfers between devices, outward(): return lax.ppermute(x, 'ctx', pairs)  13.4 us
    ppermute x15, starting transfers between devices, inward(): return lax.ppermute(x, 'ctx', pairs)  9.75 us
    pallas_call x14, Pallas kernels, call(): pl.pallas_call(body, out_shape=outs, in_specs=[VMEM] * len(operands), out...  5.05 us
  transfers between devices with their start and end apart: 26, of which 17 were waited for; matrix products, arithmetic and copies ran while one was open for 0% of the time, Pallas kernels for 1%

profile of v2, /device:TPU:0, one launch (start us, length us, event | category | flops | bytes accessed | tf_op | source)
XLA Modules:
  0.0 59.8 jit_solution(7634948891466433993)
XLA Ops:
  1.1 3.1 %collective-permute-start = (bf16[40,128]{1,0:T(8,128)(2,1)S(1)}, bf16[40,128]{1,0:T(8,128)(2,1)S(1)}, u32[]{:S(2)}, u32[]{:S(2)}) collective-permute-start(bf16[40,128]{1,0:T(8,128)(2,1)S(1)} %get-tuple-element.43), channel_id=1, source_target_pairs={{0,4},{1,5},{2,6},{3,7},{4,0},{5,1},{6,2},{7,3},{8,12},{9,13},{10,... | collective-permute-start | bytes 30728 | tf_op jit(solution)/shard_map/ppermute | solution.py:402
  4.2 2.6 %collective-permute-start.1 = (bf16[40,128]{1,0:T(8,128)(2,1)S(1)}, bf16[40,128]{1,0:T(8,128)(2,1)S(1)}, u32[]{:S(2)}, u32[]{:S(2)}) collective-permute-start(bf16[40,128]{1,0:T(8,128)(2,1)S(1)} %get-tuple-element.44), channel_id=1, source_target_pairs={{0,8},{1,9},{2,10},{3,11},{4,12},{5,13},{6,14},{7,15},{8,0},{9,1},... | collective-permute-start | bytes 30728 | tf_op jit(solution)/shard_map/ppermute | solution.py:402
  6.8 0.9 %collective-permute-start.6 = (bf16[256,128]{1,0:T(8,128)(2,1)S(1)}, bf16[256,128]{1,0:T(8,128)(2,1)S(1)}, u32[]{:S(2)}, u32[]{:S(2)}) collective-permute-start(bf16[256,128]{1,0:T(8,128)(2,1)S(1)} %get-tuple-element.48), channel_id=1, source_target_pairs={{0,4},{1,5},{2,6},{3,7},{4,0},{5,1},{6,2},{7,3},{8,12},{9,13},{10,... | collective-permute-start | bytes 196616 | tf_op jit(solution)/shard_map/ppermute | solution.py:402
  7.8 3.5 %collective-permute-start.7 = (bf16[256,128]{1,0:T(8,128)(2,1)S(1)}, bf16[256,128]{1,0:T(8,128)(2,1)S(1)}, u32[]{:S(2)}, u32[]{:S(2)}) collective-permute-start(bf16[256,128]{1,0:T(8,128)(2,1)S(1)} %get-tuple-element.49), channel_id=1, source_target_pairs={{0,8},{1,9},{2,10},{3,11},{4,12},{5,13},{6,14},{7,15},{8,0},{9,1},... | collective-permute-start | bytes 196616 | tf_op jit(solution)/shard_map/ppermute | solution.py:402
  11.3 0.9 %collective-permute-done.2.refs_3_.refs_4_ = bf16[40,128]{1,0:T(8,128)(2,1)S(1)} collective-permute-done((bf16[40,128]{1,0:T(8,128)(2,1)S(1)}, bf16[40,128]{1,0:T(8,128)(2,1)S(1)}, u32[]{:S(2)}, u32[]{:S(2)}) %collective-permute-start.2) | collective-permute-done | bytes 10272 | tf_op jit(solution)/shard_map/ppermute | solution.py:402
  12.3 1.6 %collective-permute-start.4 = (bf16[112,128]{1,0:T(8,128)(2,1)S(1)}, bf16[112,128]{1,0:T(8,128)(2,1)S(1)}, u32[]{:S(2)}, u32[]{:S(2)}) collective-permute-start(bf16[112,128]{1,0:T(8,128)(2,1)S(1)} %shard_map.138.refs_0_.refs_9_), channel_id=1, source_target_pairs={{0,2},{1,3},{2,0},{3,1},{4,6},{5,7},{6,4},{7,5},{8,10},{9,11},{10,... | collective-permute-start | bytes 86024 | tf_op jit(solution)/shard_map/ppermute | solution.py:406
  13.9 1.9 %collective-permute-done.5.refs_3_.refs_12_ = bf16[112,128]{1,0:T(8,128)(2,1)S(1)} collective-permute-done((bf16[112,128]{1,0:T(8,128)(2,1)S(1)}, bf16[112,128]{1,0:T(8,128)(2,1)S(1)}, u32[]{:S(2)}, u32[]{:S(2)}) %collective-permute-start.5) | collective-permute-done | bytes 28704 | tf_op jit(solution)/shard_map/ppermute | solution.py:406
  16.3 0.8 %collective-permute-done.3.refs_1_.refs_10_ = bf16[112,128]{1,0:T(8,128)(2,1)S(1)} collective-permute-done((bf16[112,128]{1,0:T(8,128)(2,1)S(1)}, bf16[112,128]{1,0:T(8,128)(2,1)S(1)}, u32[]{:S(2)}, u32[]{:S(2)}) %collective-permute-start.3) | collective-permute-done | bytes 28704 | tf_op jit(solution)/shard_map/ppermute | solution.py:406
  17.3 1.1 %shard_map.141 = (bf16[112,128]{1,0:T(8,128)(2,1)S(1)}, bf16[112,128]{1,0:T(8,128)(2,1)S(1)}, bf16[112,128]{1,0:T(8,128)(2,1)S(1)}, bf16[112,128]{1,0:T(8,128)(2,1)S(1)}) custom-call(bf16[384,384]{1,0:T(8,128)(2,1)S(1)} %get-tuple-element.46.refs_0_, bf16[40,128]{1,0:T(8,128)(2,1)S(1)} %get-tuple-element.42.refs_0_.refs_1_, ...), custom_call_target="tpu_custom_call" | custom-call | flops 1000000000 | bytes 1000000 | tf_op jit(solution)/shard_map/pallas_call | solution.py:30
  18.5 1.6 %collective-permute-start.10 = (bf16[112,128]{1,0:T(8,128)(2,1)S(1)}, bf16[112,128]{1,0:T(8,128)(2,1)S(1)}, u32[]{:S(2)}, u32[]{:S(2)}) collective-permute-start(bf16[112,128]{1,0:T(8,128)(2,1)S(1)} %get-tuple-element.53), channel_id=1, source_target_pairs={{0,2},{1,3},{2,0},{3,1},{4,6},{5,7},{6,4},{7,5},{8,10},{9,11},{10,... | collective-permute-start | bytes 86024 | tf_op jit(solution)/shard_map/ppermute | solution.py:406
  20.4 2.1 %collective-permute-done.10.refs_2_ = bf16[112,128]{1,0:T(8,128)(2,1)S(1)} collective-permute-done((bf16[112,128]{1,0:T(8,128)(2,1)S(1)}, bf16[112,128]{1,0:T(8,128)(2,1)S(1)}, u32[]{:S(2)}, u32[]{:S(2)}) %collective-permute-start.10) | collective-permute-done | bytes 28704 | tf_op jit(solution)/shard_map/ppermute | solution.py:406
  22.4 0.9 %collective-permute-done.11.refs_3_ = bf16[112,128]{1,0:T(8,128)(2,1)S(1)} collective-permute-done((bf16[112,128]{1,0:T(8,128)(2,1)S(1)}, bf16[112,128]{1,0:T(8,128)(2,1)S(1)}, u32[]{:S(2)}, u32[]{:S(2)}) %collective-permute-start.11) | collective-permute-done | bytes 28704 | tf_op jit(solution)/shard_map/ppermute | solution.py:406
  23.4 0.8 %shard_map.142 = (f32[48,512]{1,0:T(8,128)S(1)}, bf16[48,512]{1,0:T(8,128)(2,1)S(1)}, bf16[48,512]{1,0:T(8,128)(2,1)S(1)}, bf16[48,512]{1,0:T(8,128)(2,1)S(1)}) custom-call(bf16[112,128]{1,0:T(8,128)(2,1)S(1)} %get-tuple-element.51.refs_0_, bf16[112,128]{1,0:T(8,128)(2,1)S(1)} %collective-permute-done.9.refs_1_, ...), custom_call_target="tpu_custom_call" | custom-call | flops 1000000000 | bytes 1000000 | tf_op jit(solution)/shard_map/pallas_call | solution.py:30
  24.4 0.8 %collective-permute-start.13 = (bf16[48,512]{1,0:T(8,128)(2,1)S(1)}, bf16[48,512]{1,0:T(8,128)(2,1)S(1)}, u32[]{:S(2)}, u32[]{:S(2)}) collective-permute-start(bf16[48,512]{1,0:T(8,128)(2,1)S(1)} %get-tuple-element.57), channel_id=1, source_target_pairs={{0,2},{1,3},{2,0},{3,1},{4,6},{5,7},{6,4},{7,5},{8,10},{9,11},{10,... | collective-permute-start | bytes 147464 | tf_op jit(solution)/shard_map/ppermute | solution.py:406
  25.2 0.9 %collective-permute-start.14 = (bf16[48,512]{1,0:T(8,128)(2,1)S(1)}, bf16[48,512]{1,0:T(8,128)(2,1)S(1)}, u32[]{:S(2)}, u32[]{:S(2)}) collective-permute-start(bf16[48,512]{1,0:T(8,128)(2,1)S(1)} %get-tuple-element.58), channel_id=1, source_target_pairs={{0,3},{1,2},{2,1},{3,0},{4,7},{5,6},{6,5},{7,4},{8,11},{9,10},{10,... | collective-permute-start | bytes 147464 | tf_op jit(solution)/shard_map/ppermute | solution.py:406
  26.1 2.7 %collective-permute-done.13.refs_1_ = bf16[48,512]{1,0:T(8,128)(2,1)S(1)} collective-permute-done((bf16[48,512]{1,0:T(8,128)(2,1)S(1)}, bf16[48,512]{1,0:T(8,128)(2,1)S(1)}, u32[]{:S(2)}, u32[]{:S(2)}) %collective-permute-start.13) | collective-permute-done | bytes 49184 | tf_op jit(solution)/shard_map/ppermute | solution.py:406
  29.3 4.1 %collective-permute-done.15.refs_0_ = bf16[48,512]{1,0:T(8,128)(2,1)S(1)} collective-permute-done((bf16[48,512]{1,0:T(8,128)(2,1)S(1)}, bf16[48,512]{1,0:T(8,128)(2,1)S(1)}, u32[]{:S(2)}, u32[]{:S(2)}) %collective-permute-start.15) | collective-permute-done | bytes 49184 | tf_op jit(solution)/shard_map/ppermute | solution.py:402
  33.4 1.3 %collective-permute-start.16 = (bf16[48,512]{1,0:T(8,128)(2,1)S(1)}, bf16[48,512]{1,0:T(8,128)(2,1)S(1)}, u32[]{:S(2)}, u32[]{:S(2)}) collective-permute-start(bf16[48,512]{1,0:T(8,128)(2,1)S(1)} %get-tuple-element.62), channel_id=1, source_target_pairs={{0,8},{1,9},{2,10},{3,11},{4,12},{5,13},{6,14},{7,15},{8,0},{9,1},... | collective-permute-start | bytes 147464 | tf_op jit(solution)/shard_map/ppermute | solution.py:402
  34.7 4.1 %collective-permute-done.16.refs_0_ = bf16[48,512]{1,0:T(8,128)(2,1)S(1)} collective-permute-done((bf16[48,512]{1,0:T(8,128)(2,1)S(1)}, bf16[48,512]{1,0:T(8,128)(2,1)S(1)}, u32[]{:S(2)}, u32[]{:S(2)}) %collective-permute-start.16) | collective-permute-done | bytes 49184 | tf_op jit(solution)/shard_map/ppermute | solution.py:402
  39.0 1.1 %collective-permute-start.19 = (bf16[48,512]{1,0:T(8,128)(2,1)S(1)}, bf16[48,512]{1,0:T(8,128)(2,1)S(1)}, u32[]{:S(2)}, u32[]{:S(2)}) collective-permute-start(bf16[48,512]{1,0:T(8,128)(2,1)S(1)} %get-tuple-element.64), channel_id=1, source_target_pairs={{0,3},{1,2},{2,1},{3,0},{4,7},{5,6},{6,5},{7,4},{8,11},{9,10},{10,... | collective-permute-start | bytes 147464 | tf_op jit(solution)/shard_map/ppermute | solution.py:406
  40.1 1.1 %collective-permute-start.18 = (bf16[48,512]{1,0:T(8,128)(2,1)S(1)}, bf16[48,512]{1,0:T(8,128)(2,1)S(1)}, u32[]{:S(2)}, u32[]{:S(2)}) collective-permute-start(bf16[48,512]{1,0:T(8,128)(2,1)S(1)} %get-tuple-element.64), channel_id=1, source_target_pairs={{0,2},{1,3},{2,0},{3,1},{4,6},{5,7},{6,4},{7,5},{8,10},{9,11},{10,... | collective-permute-start | bytes 147464 | tf_op jit(solution)/shard_map/ppermute | solution.py:406
  41.2 0.7 %shard_map.146 = (f32[48,768]{1,0:T(8,128)S(1)}, f32[48,768]{1,0:T(8,128)S(1)}, f32[48,128]{1,0:T(8,128)S(1)}) custom-call(bf16[1,2048,768]{2,1,0:T(8,128)(2,1)S(1)} %copy-done, bf16[1,2048,768]{2,1,0:T(8,128)(2,1)S(1)} %copy-done.1, bf16[1,2048]{1,0:T(2,128)(2,1)S(1)} %reshape.3.gain, f32[48,512]{1,0:T(8,128)S(1)} %get-tuple-element.63.refs_0_, ...), custom_call_target="tpu_custom_call" | custom-call | flops 1000000000 | bytes 1000000 | tf_op jit(solution)/shard_map/pallas_call | solution.py:30
  41.9 0.7 %collective-permute-done.19.refs_3_ = bf16[48,512]{1,0:T(8,128)(2,1)S(1)} collective-permute-done((bf16[48,512]{1,0:T(8,128)(2,1)S(1)}, bf16[48,512]{1,0:T(8,128)(2,1)S(1)}, u32[]{:S(2)}, u32[]{:S(2)}) %collective-permute-start.19) | collective-permute-done | bytes 49184 | tf_op jit(solution)/shard_map/ppermute | solution.py:406
  42.6 1.7 %collective-permute-done.18.refs_2_ = bf16[48,512]{1,0:T(8,128)(2,1)S(1)} collective-permute-done((bf16[48,512]{1,0:T(8,128)(2,1)S(1)}, bf16[48,512]{1,0:T(8,128)(2,1)S(1)}, u32[]{:S(2)}, u32[]{:S(2)}) %collective-permute-start.18) | collective-permute-done | bytes 49184 | tf_op jit(solution)/shard_map/ppermute | solution.py:406
  44.3 1.3 %shard_map.147 = (f32[192,128]{1,0:T(8,128)S(1)}, bf16[192,128]{1,0:T(8,128)(2,1)S(1)}, bf16[192,128]{1,0:T(8,128)(2,1)S(1)}, bf16[192,128]{1,0:T(8,128)(2,1)S(1)}, f32[3,2048]{1,0:T(4,128)S(1)}) custom-call(bf16[1,2048,768]{2,1,0:T(8,128)(2,1)S(1)} %copy-done, bf16[1,2048,768]{2,1,0:T(8,128)(2,1)S(1)} %copy-done.1, bf16[1,768,2048]{2,1,0:T(8,128)(2,1)S(1)} %copy-done.2, ...), custom_call_target="tpu_custom_call" | custom-call | flops 1000000000 | bytes 1000000 | tf_op jit(solution)/shard_map/pallas_call | solution.py:30
  45.7 1.1 %collective-permute-start.21 = (bf16[192,128]{1,0:T(8,128)(2,1)S(1)}, bf16[192,128]{1,0:T(8,128)(2,1)S(1)}, u32[]{:S(2)}, u32[]{:S(2)}) collective-permute-start(bf16[192,128]{1,0:T(8,128)(2,1)S(1)} %get-tuple-element.71), channel_id=1, source_target_pairs={{0,2},{1,3},{2,0},{3,1},{4,6},{5,7},{6,4},{7,5},{8,10},{9,11},{10,... | collective-permute-start | bytes 147464 | tf_op jit(solution)/shard_map/ppermute | solution.py:406
  46.7 0.8 %collective-permute-start.22 = (bf16[192,128]{1,0:T(8,128)(2,1)S(1)}, bf16[192,128]{1,0:T(8,128)(2,1)S(1)}, u32[]{:S(2)}, u32[]{:S(2)}) collective-permute-start(bf16[192,128]{1,0:T(8,128)(2,1)S(1)} %get-tuple-element.72), channel_id=1, source_target_pairs={{0,3},{1,2},{2,1},{3,0},{4,7},{5,6},{6,5},{7,4},{8,11},{9,10},{10,... | collective-permute-start | bytes 147464 | tf_op jit(solution)/shard_map/ppermute | solution.py:406
  47.5 2.4 %collective-permute-done.21.refs_2_ = bf16[192,128]{1,0:T(8,128)(2,1)S(1)} collective-permute-done((bf16[192,128]{1,0:T(8,128)(2,1)S(1)}, bf16[192,128]{1,0:T(8,128)(2,1)S(1)}, u32[]{:S(2)}, u32[]{:S(2)}) %collective-permute-start.21) | collective-permute-done | bytes 49184 | tf_op jit(solution)/shard_map/ppermute | solution.py:406
  49.9 0.7 %collective-permute-done.22.refs_3_ = bf16[192,128]{1,0:T(8,128)(2,1)S(1)} collective-permute-done((bf16[192,128]{1,0:T(8,128)(2,1)S(1)}, bf16[192,128]{1,0:T(8,128)(2,1)S(1)}, u32[]{:S(2)}, u32[]{:S(2)}) %collective-permute-start.22) | collective-permute-done | bytes 49184 | tf_op jit(solution)/shard_map/ppermute | solution.py:406
  50.8 2.9 %collective-permute-start.24 = (bf16[48,128]{1,0:T(8,128)(2,1)S(1)}, bf16[48,128]{1,0:T(8,128)(2,1)S(1)}, u32[]{:S(2)}, u32[]{:S(2)}) collective-permute-start(bf16[48,128]{1,0:T(8,128)(2,1)S(1)} %get-tuple-element.75), channel_id=1, source_target_pairs={{0,8},{1,9},{2,10},{3,11},{4,12},{5,13},{6,14},{7,15},{8,0},{9,1},... | collective-permute-start | bytes 36872 | tf_op jit(solution)/shard_map/ppermute | solution.py:402
  53.7 1.4 %collective-permute-start.25 = (bf16[48,128]{1,0:T(8,128)(2,1)S(1)}, bf16[48,128]{1,0:T(8,128)(2,1)S(1)}, u32[]{:S(2)}, u32[]{:S(2)}) collective-permute-start(bf16[48,128]{1,0:T(8,128)(2,1)S(1)} %get-tuple-element.76), channel_id=1, source_target_pairs={{0,12},{1,13},{2,14},{3,15},{4,8},{5,9},{6,10},{7,11},{8,4},{9,5},... | collective-permute-start | bytes 36872 | tf_op jit(solution)/shard_map/ppermute | solution.py:402
  55.4 3.8 %collective-permute-done.25.refs_2_ = bf16[48,128]{1,0:T(8,128)(2,1)S(1)} collective-permute-done((bf16[48,128]{1,0:T(8,128)(2,1)S(1)}, bf16[48,128]{1,0:T(8,128)(2,1)S(1)}, u32[]{:S(2)}, u32[]{:S(2)}) %collective-permute-start.25) | collective-permute-done | bytes 12320 | tf_op jit(solution)/shard_map/ppermute | solution.py:402
  (61 shorter events, 3.6 us)
Async XLA Ops:
  0.0 6.7 %copy-start.5 = (bf16[128,512]{1,0:T(8,128)(2,1)S(1)}, bf16[128,512]{1,0:T(8,128)(2,1)}, u32[]{:S(2)}) copy-start(bf16[128,512]{1,0:T(8,128)(2,1)} %values.1) | copy-start | bytes 393220
  0.0 6.7 %copy-start.4 = (bf16[128,512]{1,0:T(8,128)(2,1)S(1)}, bf16[128,512]{1,0:T(8,128)(2,1)}, u32[]{:S(2)}) copy-start(bf16[128,512]{1,0:T(8,128)(2,1)} %keys.1) | copy-start | bytes 393220
  1.1 10.2 %collective-permute-start = (bf16[40,128]{1,0:T(8,128)(2,1)S(1)}, bf16[40,128]{1,0:T(8,128)(2,1)S(1)}, u32[]{:S(2)}, u32[]{:S(2)}) collective-permute-start(bf16[40,128]{1,0:T(8,128)(2,1)S(1)} %get-tuple-element.43), channel_id=1, source_target_pairs={{0,4},{1,5},{2,6},{3,7},{4,0},{5,1},{6,2},{7,3},{8,12},{9,13},{10,... | collective-permute-start | bytes 30728 | tf_op jit(solution)/shard_map/ppermute | solution.py:402
  4.2 7.1 %collective-permute-start.1 = (bf16[40,128]{1,0:T(8,128)(2,1)S(1)}, bf16[40,128]{1,0:T(8,128)(2,1)S(1)}, u32[]{:S(2)}, u32[]{:S(2)}) collective-permute-start(bf16[40,128]{1,0:T(8,128)(2,1)S(1)} %get-tuple-element.44), channel_id=1, source_target_pairs={{0,8},{1,9},{2,10},{3,11},{4,12},{5,13},{6,14},{7,15},{8,0},{9,1},... | collective-permute-start | bytes 30728 | tf_op jit(solution)/shard_map/ppermute | solution.py:402
  6.8 5.5 %collective-permute-start.2 = (bf16[40,128]{1,0:T(8,128)(2,1)S(1)}, bf16[40,128]{1,0:T(8,128)(2,1)S(1)}, u32[]{:S(2)}, u32[]{:S(2)}) collective-permute-start(bf16[40,128]{1,0:T(8,128)(2,1)S(1)} %get-tuple-element.45), channel_id=1, source_target_pairs={{0,12},{1,13},{2,14},{3,15},{4,8},{5,9},{6,10},{7,11},{8,4},{9,5},... | collective-permute-start | bytes 30728 | tf_op jit(solution)/shard_map/ppermute | solution.py:402
  6.8 10.2 %collective-permute-start.6 = (bf16[256,128]{1,0:T(8,128)(2,1)S(1)}, bf16[256,128]{1,0:T(8,128)(2,1)S(1)}, u32[]{:S(2)}, u32[]{:S(2)}) collective-permute-start(bf16[256,128]{1,0:T(8,128)(2,1)S(1)} %get-tuple-element.48), channel_id=1, source_target_pairs={{0,4},{1,5},{2,6},{3,7},{4,0},{5,1},{6,2},{7,3},{8,12},{9,13},{10,... | collective-permute-start | bytes 196616 | tf_op jit(solution)/shard_map/ppermute | solution.py:402
  7.8 9.3 %collective-permute-start.7 = (bf16[256,128]{1,0:T(8,128)(2,1)S(1)}, bf16[256,128]{1,0:T(8,128)(2,1)S(1)}, u32[]{:S(2)}, u32[]{:S(2)}) collective-permute-start(bf16[256,128]{1,0:T(8,128)(2,1)S(1)} %get-tuple-element.49), channel_id=1, source_target_pairs={{0,8},{1,9},{2,10},{3,11},{4,12},{5,13},{6,14},{7,15},{8,0},{9,1},... | collective-permute-start | bytes 196616 | tf_op jit(solution)/shard_map/ppermute | solution.py:402
  11.3 6.1 %collective-permute-start.8 = (bf16[256,128]{1,0:T(8,128)(2,1)S(1)}, bf16[256,128]{1,0:T(8,128)(2,1)S(1)}, u32[]{:S(2)}, u32[]{:S(2)}) collective-permute-start(bf16[256,128]{1,0:T(8,128)(2,1)S(1)} %get-tuple-element.50), channel_id=1, source_target_pairs={{0,12},{1,13},{2,14},{3,15},{4,8},{5,9},{6,10},{7,11},{8,4},{9,5},... | collective-permute-start | bytes 196616 | tf_op jit(solution)/shard_map/ppermute | solution.py:402
  12.2 11.2 %copy-start.3 = (bf16[256,2048]{1,0:T(8,128)(2,1)S(1)}, bf16[256,2048]{1,0:T(8,128)(2,1)}, u32[]{:S(2)}) copy-start(bf16[256,2048]{1,0:T(8,128)(2,1)} %refs_4_.1) | copy-start | bytes 3145732
  12.2 11.2 %copy-start.7 = (bf16[3,2048]{1,0:T(4,128)(2,1)S(1)}, bf16[3,2048]{1,0:T(4,128)(2,1)}, u32[]{:S(2)}) copy-start(bf16[3,2048]{1,0:T(4,128)(2,1)} %refs_5_.1) | copy-start | bytes 36868
  12.2 3.6 %collective-permute-start.5 = (bf16[112,128]{1,0:T(8,128)(2,1)S(1)}, bf16[112,128]{1,0:T(8,128)(2,1)S(1)}, u32[]{:S(2)}, u32[]{:S(2)}) collective-permute-start(bf16[112,128]{1,0:T(8,128)(2,1)S(1)} %shard_map.138.refs_0_.refs_9_), channel_id=1, source_target_pairs={{0,3},{1,2},{2,1},{3,0},{4,7},{5,6},{6,5},{7,4},{8,11},{9,10},{10,... | collective-permute-start | bytes 86024 | tf_op jit(solution)/shard_map/ppermute | solution.py:406
  12.3 3.9 %collective-permute-start.4 = (bf16[112,128]{1,0:T(8,128)(2,1)S(1)}, bf16[112,128]{1,0:T(8,128)(2,1)S(1)}, u32[]{:S(2)}, u32[]{:S(2)}) collective-permute-start(bf16[112,128]{1,0:T(8,128)(2,1)S(1)} %shard_map.138.refs_0_.refs_9_), channel_id=1, source_target_pairs={{0,2},{1,3},{2,0},{3,1},{4,6},{5,7},{6,4},{7,5},{8,10},{9,11},{10,... | collective-permute-start | bytes 86024 | tf_op jit(solution)/shard_map/ppermute | solution.py:406
  15.8 1.2 %collective-permute-start.3 = (bf16[112,128]{1,0:T(8,128)(2,1)S(1)}, bf16[112,128]{1,0:T(8,128)(2,1)S(1)}, u32[]{:S(2)}, u32[]{:S(2)}) collective-permute-start(bf16[112,128]{1,0:T(8,128)(2,1)S(1)} %shard_map.138.refs_0_.refs_9_), channel_id=1, source_target_pairs={{0,1},{1,0},{2,3},{3,2},{4,5},{5,4},{6,7},{7,6},{8,9},{9,8},{10,11... | collective-permute-start | bytes 86024 | tf_op jit(solution)/shard_map/ppermute | solution.py:406
  18.5 1.9 %collective-permute-start.9 = (bf16[112,128]{1,0:T(8,128)(2,1)S(1)}, bf16[112,128]{1,0:T(8,128)(2,1)S(1)}, u32[]{:S(2)}, u32[]{:S(2)}) collective-permute-start(bf16[112,128]{1,0:T(8,128)(2,1)S(1)} %get-tuple-element.52), channel_id=1, source_target_pairs={{0,1},{1,0},{2,3},{3,2},{4,5},{5,4},{6,7},{7,6},{8,9},{9,8},{10,11... | collective-permute-start | bytes 86024 | tf_op jit(solution)/shard_map/ppermute | solution.py:406
  18.5 3.9 %collective-permute-start.10 = (bf16[112,128]{1,0:T(8,128)(2,1)S(1)}, bf16[112,128]{1,0:T(8,128)(2,1)S(1)}, u32[]{:S(2)}, u32[]{:S(2)}) collective-permute-start(bf16[112,128]{1,0:T(8,128)(2,1)S(1)} %get-tuple-element.53), channel_id=1, source_target_pairs={{0,2},{1,3},{2,0},{3,1},{4,6},{5,7},{6,4},{7,5},{8,10},{9,11},{10,... | collective-permute-start | bytes 86024 | tf_op jit(solution)/shard_map/ppermute | solution.py:406
  20.1 3.3 %collective-permute-start.11 = (bf16[112,128]{1,0:T(8,128)(2,1)S(1)}, bf16[112,128]{1,0:T(8,128)(2,1)S(1)}, u32[]{:S(2)}, u32[]{:S(2)}) collective-permute-start(bf16[112,128]{1,0:T(8,128)(2,1)S(1)} %get-tuple-element.54), channel_id=1, source_target_pairs={{0,3},{1,2},{2,1},{3,0},{4,7},{5,6},{6,5},{7,4},{8,11},{9,10},{10,... | collective-permute-start | bytes 86024 | tf_op jit(solution)/shard_map/ppermute | solution.py:406
  24.2 1.9 %collective-permute-start.12 = (bf16[48,512]{1,0:T(8,128)(2,1)S(1)}, bf16[48,512]{1,0:T(8,128)(2,1)S(1)}, u32[]{:S(2)}, u32[]{:S(2)}) collective-permute-start(bf16[48,512]{1,0:T(8,128)(2,1)S(1)} %get-tuple-element.56), channel_id=1, source_target_pairs={{0,1},{1,0},{2,3},{3,2},{4,5},{5,4},{6,7},{7,6},{8,9},{9,8},{10,11... | collective-permute-start | bytes 147464 | tf_op jit(solution)/shard_map/ppermute | solution.py:406
  24.4 4.4 %collective-permute-start.13 = (bf16[48,512]{1,0:T(8,128)(2,1)S(1)}, bf16[48,512]{1,0:T(8,128)(2,1)S(1)}, u32[]{:S(2)}, u32[]{:S(2)}) collective-permute-start(bf16[48,512]{1,0:T(8,128)(2,1)S(1)} %get-tuple-element.57), channel_id=1, source_target_pairs={{0,2},{1,3},{2,0},{3,1},{4,6},{5,7},{6,4},{7,5},{8,10},{9,11},{10,... | collective-permute-start | bytes 147464 | tf_op jit(solution)/shard_map/ppermute | solution.py:406
  25.2 4.0 %collective-permute-start.14 = (bf16[48,512]{1,0:T(8,128)(2,1)S(1)}, bf16[48,512]{1,0:T(8,128)(2,1)S(1)}, u32[]{:S(2)}, u32[]{:S(2)}) collective-permute-start(bf16[48,512]{1,0:T(8,128)(2,1)S(1)} %get-tuple-element.58), channel_id=1, source_target_pairs={{0,3},{1,2},{2,1},{3,0},{4,7},{5,6},{6,5},{7,4},{8,11},{9,10},{10,... | collective-permute-start | bytes 147464 | tf_op jit(solution)/shard_map/ppermute | solution.py:406
  29.3 4.2 %collective-permute-start.15 = (bf16[48,512]{1,0:T(8,128)(2,1)S(1)}, bf16[48,512]{1,0:T(8,128)(2,1)S(1)}, u32[]{:S(2)}, u32[]{:S(2)}) collective-permute-start(bf16[48,512]{1,0:T(8,128)(2,1)S(1)} %get-tuple-element.60), channel_id=1, source_target_pairs={{0,4},{1,5},{2,6},{3,7},{4,0},{5,1},{6,2},{7,3},{8,12},{9,13},{10,... | collective-permute-start | bytes 147464 | tf_op jit(solution)/shard_map/ppermute | solution.py:402
  33.4 7.8 %copy-start = (bf16[1,2048,768]{2,1,0:T(8,128)(2,1)S(1)}, bf16[1,2048,768]{2,1,0:T(8,128)(2,1)}, u32[]{:S(2)}) copy-start(bf16[1,2048,768]{2,1,0:T(8,128)(2,1)} %gate.3) | copy-start | bytes 9437188
  33.4 7.8 %copy-start.1 = (bf16[1,2048,768]{2,1,0:T(8,128)(2,1)S(1)}, bf16[1,2048,768]{2,1,0:T(8,128)(2,1)}, u32[]{:S(2)}) copy-start(bf16[1,2048,768]{2,1,0:T(8,128)(2,1)} %up.3) | copy-start | bytes 9437188
  33.4 5.3 %collective-permute-start.16 = (bf16[48,512]{1,0:T(8,128)(2,1)S(1)}, bf16[48,512]{1,0:T(8,128)(2,1)S(1)}, u32[]{:S(2)}, u32[]{:S(2)}) collective-permute-start(bf16[48,512]{1,0:T(8,128)(2,1)S(1)} %get-tuple-element.62), channel_id=1, source_target_pairs={{0,8},{1,9},{2,10},{3,11},{4,12},{5,13},{6,14},{7,15},{8,0},{9,1},... | collective-permute-start | bytes 147464 | tf_op jit(solution)/shard_map/ppermute | solution.py:402
  38.8 2.4 %collective-permute-start.17 = (bf16[48,512]{1,0:T(8,128)(2,1)S(1)}, bf16[48,512]{1,0:T(8,128)(2,1)S(1)}, u32[]{:S(2)}, u32[]{:S(2)}) collective-permute-start(bf16[48,512]{1,0:T(8,128)(2,1)S(1)} %get-tuple-element.64), channel_id=1, source_target_pairs={{0,1},{1,0},{2,3},{3,2},{4,5},{5,4},{6,7},{7,6},{8,9},{9,8},{10,11... | collective-permute-start | bytes 147464 | tf_op jit(solution)/shard_map/ppermute | solution.py:406
  39.0 3.6 %collective-permute-start.19 = (bf16[48,512]{1,0:T(8,128)(2,1)S(1)}, bf16[48,512]{1,0:T(8,128)(2,1)S(1)}, u32[]{:S(2)}, u32[]{:S(2)}) collective-permute-start(bf16[48,512]{1,0:T(8,128)(2,1)S(1)} %get-tuple-element.64), channel_id=1, source_target_pairs={{0,3},{1,2},{2,1},{3,0},{4,7},{5,6},{6,5},{7,4},{8,11},{9,10},{10,... | collective-permute-start | bytes 147464 | tf_op jit(solution)/shard_map/ppermute | solution.py:406
  40.1 4.2 %collective-permute-start.18 = (bf16[48,512]{1,0:T(8,128)(2,1)S(1)}, bf16[48,512]{1,0:T(8,128)(2,1)S(1)}, u32[]{:S(2)}, u32[]{:S(2)}) collective-permute-start(bf16[48,512]{1,0:T(8,128)(2,1)S(1)} %get-tuple-element.64), channel_id=1, source_target_pairs={{0,2},{1,3},{2,0},{3,1},{4,6},{5,7},{6,4},{7,5},{8,10},{9,11},{10,... | collective-permute-start | bytes 147464 | tf_op jit(solution)/shard_map/ppermute | solution.py:406
  45.6 1.9 %collective-permute-start.20 = (bf16[192,128]{1,0:T(8,128)(2,1)S(1)}, bf16[192,128]{1,0:T(8,128)(2,1)S(1)}, u32[]{:S(2)}, u32[]{:S(2)}) collective-permute-start(bf16[192,128]{1,0:T(8,128)(2,1)S(1)} %get-tuple-element.70), channel_id=1, source_target_pairs={{0,1},{1,0},{2,3},{3,2},{4,5},{5,4},{6,7},{7,6},{8,9},{9,8},{10,11... | collective-permute-start | bytes 147464 | tf_op jit(solution)/shard_map/ppermute | solution.py:406
  45.7 4.2 %collective-permute-start.21 = (bf16[192,128]{1,0:T(8,128)(2,1)S(1)}, bf16[192,128]{1,0:T(8,128)(2,1)S(1)}, u32[]{:S(2)}, u32[]{:S(2)}) collective-permute-start(bf16[192,128]{1,0:T(8,128)(2,1)S(1)} %get-tuple-element.71), channel_id=1, source_target_pairs={{0,2},{1,3},{2,0},{3,1},{4,6},{5,7},{6,4},{7,5},{8,10},{9,11},{10,... | collective-permute-start | bytes 147464 | tf_op jit(solution)/shard_map/ppermute | solution.py:406
  46.7 3.9 %collective-permute-start.22 = (bf16[192,128]{1,0:T(8,128)(2,1)S(1)}, bf16[192,128]{1,0:T(8,128)(2,1)S(1)}, u32[]{:S(2)}, u32[]{:S(2)}) collective-permute-start(bf16[192,128]{1,0:T(8,128)(2,1)S(1)} %get-tuple-element.72), channel_id=1, source_target_pairs={{0,3},{1,2},{2,1},{3,0},{4,7},{5,6},{6,5},{7,4},{8,11},{9,10},{10,... | collective-permute-start | bytes 147464 | tf_op jit(solution)/shard_map/ppermute | solution.py:406
  50.7 4.5 %collective-permute-start.23 = (bf16[48,128]{1,0:T(8,128)(2,1)S(1)}, bf16[48,128]{1,0:T(8,128)(2,1)S(1)}, u32[]{:S(2)}, u32[]{:S(2)}) collective-permute-start(bf16[48,128]{1,0:T(8,128)(2,1)S(1)} %get-tuple-element.74), channel_id=1, source_target_pairs={{0,4},{1,5},{2,6},{3,7},{4,0},{5,1},{6,2},{7,3},{8,12},{9,13},{10,... | collective-permute-start | bytes 36872 | tf_op jit(solution)/shard_map/ppermute | solution.py:402
  50.8 4.6 %collective-permute-start.24 = (bf16[48,128]{1,0:T(8,128)(2,1)S(1)}, bf16[48,128]{1,0:T(8,128)(2,1)S(1)}, u32[]{:S(2)}, u32[]{:S(2)}) collective-permute-start(bf16[48,128]{1,0:T(8,128)(2,1)S(1)} %get-tuple-element.75), channel_id=1, source_target_pairs={{0,8},{1,9},{2,10},{3,11},{4,12},{5,13},{6,14},{7,15},{8,0},{9,1},... | collective-permute-start | bytes 36872 | tf_op jit(solution)/shard_map/ppermute | solution.py:402
  53.7 5.5 %collective-permute-start.25 = (bf16[48,128]{1,0:T(8,128)(2,1)S(1)}, bf16[48,128]{1,0:T(8,128)(2,1)S(1)}, u32[]{:S(2)}, u32[]{:S(2)}) collective-permute-start(bf16[48,128]{1,0:T(8,128)(2,1)S(1)} %get-tuple-element.76), channel_id=1, source_target_pairs={{0,12},{1,13},{2,14},{3,15},{4,8},{5,9},{6,10},{7,11},{8,4},{9,5},... | collective-permute-start | bytes 36872 | tf_op jit(solution)/shard_map/ppermute | solution.py:402
  (7 other events, 12.9 us)
